TPU v7x, 32 devices: a whole 2x2x4 slice. The times are simulated.
32 devices in a mesh: seq: 8 (over z, y), mp: 4 (over x, core).
Axes of the slice: x: 2, y: 2, z: 4, core: 2. Of those that a mesh axis runs over, the one named last changes fastest.
Arguments:
- gate_in: bfloat16 [8192, 1024], P('seq', 'mp'), may hold values from -5 to 5
- value_in: bfloat16 [8192, 1024], P('seq', 'mp'), may hold values from -5 to 5
- out_gate: bfloat16 [8192, 1024], P('seq', 'mp'), may hold values from -10 to 10
- filter_taps: bfloat16 [4096, 1024], P('seq', 'mp'), may hold values from -0.09375 to 0.09375
- skip_gain: float32 [1024], P('mp'), may hold values from -4 to 4
Outputs:
- output: bfloat16 [8192, 1024], P('seq', 'mp')
All inputs are finite; a program needn't handle non-finite values.
Results may differ from a plain program's by a relative error of at most 0.009.
Values may be sent and summed in bfloat16 or wider, within the bound.
No kernel may reach another device: no remote copies, remote signals or barrier semaphores. Data moves between devices by JAX's collectives and lax.ppermute only.
A program may use at most 64 MiB of HBM per device.

v0:
```python
import math

import jax
import jax.numpy as jnp
from jax import lax
from jax.sharding import PartitionSpec as P

C = 1024
K = 4096
P_SIZE = 128


def shortened(shard):
    return jax.tree.map(lambda a: a.astype(jnp.bfloat16) if a.dtype == jnp.float32 else a, shard)


def dft_tables(block):
    frame_len = 2 * block
    sample = lax.iota(jnp.int32, frame_len)[:, None]
    frequency = lax.iota(jnp.int32, block)[None, :]
    angles = (sample * frequency % frame_len).astype(jnp.float32) * (2.0 * math.pi / frame_len)
    alternate = jnp.where(sample % 2 == 0, 1.0, -1.0).astype(jnp.float32)
    forward = jnp.concatenate(
        [jnp.cos(angles), jnp.where(frequency == 0, alternate, -jnp.sin(angles))], axis=1
    )
    later = block + lax.iota(jnp.int32, block)[None, :]
    column = lax.iota(jnp.int32, block)[:, None]
    back_angles = (column * later % frame_len).astype(jnp.float32) * (2.0 * math.pi / frame_len)
    back_sign = jnp.where(later % 2 == 0, 1.0, -1.0).astype(jnp.float32)
    inv_real = jnp.where(column == 0, 1.0, 2.0 * jnp.cos(back_angles)) / frame_len
    inv_imag = jnp.where(column == 0, back_sign, -2.0 * jnp.sin(back_angles)) / frame_len
    backward = jnp.concatenate([inv_real, inv_imag], axis=0)
    return (forward, backward)


def split_table(table):
    upper_part = table.astype(jnp.bfloat16)
    lower_part = (table - upper_part.astype(jnp.float32)).astype(jnp.bfloat16)
    return (upper_part, lower_part)


def transform_rows(form, data, table):
    upper_part, lower_part = split_table(table)
    first = jnp.einsum(form, data, upper_part, preferred_element_type=jnp.float32)
    return first + jnp.einsum(form, data, lower_part, preferred_element_type=jnp.float32)


def filter_spectra(portion):
    forward, backward = dft_tables(P_SIZE)
    channels = portion.shape[1]
    segments = portion.reshape(-1, P_SIZE, channels)
    return transform_rows("snc,nf->scf", segments, forward[:P_SIZE])


def convolve(window, filter_spec):
    forward, backward = dft_tables(P_SIZE)
    channels = window.shape[1]
    blocks = window.reshape(-1, P_SIZE, channels)
    frames = jnp.concatenate([blocks[:-1], blocks[1:]], axis=1)
    spectra = transform_rows("mnc,nf->mcf", frames, forward)
    frame_count = spectra.shape[0]
    seg_count = filter_spec.shape[0]
    features = channels * 2 * P_SIZE
    lhs_data = spectra.reshape(1, frame_count, features)
    spec_real = filter_spec[..., :P_SIZE]
    spec_imag = filter_spec[..., P_SIZE:]
    kernel_real = jnp.concatenate([spec_real, spec_real], axis=-1)
    kernel_imag = jnp.concatenate([spec_imag, spec_imag], axis=-1)
    kernel = jnp.stack([kernel_real, kernel_imag], axis=-1)[::-1].reshape(
        seg_count, 1, features * 2
    )
    merged = lax.conv_general_dilated(
        lhs_data,
        kernel,
        (1,),
        "VALID",
        dimension_numbers=("NWC", "WIO", "NWC"),
        feature_group_count=features,
        precision=lax.Precision.HIGH,
    )
    merged = merged.reshape(-1, channels, 2 * P_SIZE, 2)
    with_real = merged[..., 0]
    with_imag = merged[..., 1]
    first_col = lax.iota(jnp.int32, P_SIZE) == 0
    out_real = with_real[..., :P_SIZE] - jnp.where(first_col, 0.0, with_imag[..., P_SIZE:])
    out_imag = jnp.where(
        first_col, with_imag[..., P_SIZE:], with_imag[..., :P_SIZE] + with_real[..., P_SIZE:]
    )
    joined = jnp.concatenate([out_real, out_imag], axis=-1)
    result = jnp.einsum("bcf,fn->bnc", joined, backward, precision=lax.Precision.HIGH)
    return result.reshape(-1, channels)


def local(gate_in, value_in, out_gate, filter_taps, skip_gain):
    gated = (gate_in.astype(jnp.float32) * value_in.astype(jnp.float32)).astype(jnp.bfloat16)
    by_channel, taps_channel = (
        lax.all_to_all(gated, "seq", split_axis=1, concat_axis=0, tiled=True),
        lax.all_to_all(filter_taps, "seq", split_axis=1, concat_axis=0, tiled=True),
    )
    leading = jnp.zeros((K, by_channel.shape[1]), jnp.bfloat16)
    window = jnp.concatenate([leading, by_channel], axis=0)
    filter_spec = filter_spectra(taps_channel)
    channel_result = convolve(window, filter_spec)
    convolved = lax.all_to_all(
        shortened(channel_result), "seq", split_axis=0, concat_axis=1, tiled=True
    ).astype(channel_result.dtype)
    gated_out = out_gate.astype(jnp.float32) * (
        convolved + skip_gain[None, :] * gated.astype(jnp.float32)
    )
    squares = jnp.sum(gated_out * gated_out, axis=1)
    totals = lax.psum(squares, "mp")
    return (gated_out / jnp.sqrt(totals[:, None] / C + 1e-05)).astype(jnp.bfloat16)


def solution(mesh):
    return jax.shard_map(
        local,
        mesh=mesh,
        in_specs=(P("seq", "mp"), P("seq", "mp"), P("seq", "mp"), P("seq", "mp"), P("mp")),
        out_specs=P("seq", "mp"),
        check_vma=False,
    )
```

profile of v0, /device:TPU:0, one launch (start us, length us, event | category | flops | bytes accessed | tf_op | source)
XLA Modules:
  0.0 116.8 jit_solution(7385291772707953139)
XLA Ops:
  0.0 0.0 copy-start
  0.0 1.9 %copy.17 = bf16[512,256]{0,1:T(8,128)(2,1)} copy(bf16[512,256]{1,0:T(8,128)(2,1)} %param.8) | data formatting | bytes 524288 | tf_op args[3]
  1.9 7.3 %all-to-all-start.1 = ((bf16[512,8,32]{0,2,1:T(8,128)(2,1)}), bf16[512,8,32]{0,2,1:T(8,128)(2,1)S(1)}, u32[]{:S(2)}, u32[]{:S(2)}) async-start(bf16[512,8,32]{0,2,1:T(8,128)(2,1)} %bitcast.5), calls=%async_computation.1 | async-start | bytes 524288 | tf_op jit(solution)/shard_map/all_to_all | solution.py:98
  9.2 1.2 %copy.12 = bf16[1024,256]{0,1:T(8,128)(2,1)S(1)} copy(bf16[1024,256]{1,0:T(8,128)(2,1)} %param.5) | data formatting | bytes 1048576 | tf_op args[0]
  10.5 0.0 copy-done
  10.5 0.2 copy.13
  10.7 0.5 negate_select_fusion.2
  11.2 0.3 select_multiply_fusion.1
  11.5 1.0 multiply_convert_fusion
  12.5 5.6 %all-to-all-done.1 = bf16[512,8,32]{0,2,1:T(8,128)(2,1)S(1)} async-done(((bf16[512,8,32]{0,2,1:T(8,128)(2,1)}), bf16[512,8,32]{0,2,1:T(8,128)(2,1)S(1)}, u32[]{:S(2)}, u32[]{:S(2)}) %all-to-all-start.1) | async-done | bytes 262176 | tf_op jit(solution)/shard_map/all_to_all | solution.py:98
  18.1 3.6 %all-to-all-start = ((bf16[1024,8,32]{0,2,1:T(8,128)(2,1)}), bf16[1024,8,32]{0,2,1:T(8,128)(2,1)S(1)}, u32[]{:S(2)}, u32[]{:S(2)}) async-start(bf16[1024,8,32]{0,2,1:T(8,128)(2,1)} %bitcast.1), calls=%async_computation | async-start | bytes 1048576 | tf_op jit(solution)/shard_map/all_to_all | solution.py:97
  21.7 0.1 copy.18
  21.8 0.2 reshape.98
  22.0 0.1 copy.19
  22.1 0.3 fusion.33
  22.4 0.3 fusion.39
  22.7 0.2 add_bitcast_fusion
  22.9 0.1 fusion.50
  23.0 0.1 maximum_bitcast_fusion
  23.1 0.1 maximum_bitcast_fusion.1
  23.2 0.1 pad_maximum_fusion
  23.3 1.5 %rev.3 = f32[32,32,256,2]{2,1,0,3:T(8,128)} reverse(f32[32,32,256,2]{2,1,0,3:T(8,128)S(1)} %pad_maximum_fusion), dimensions={0} | reverse | bytes 4194304 | tf_op jit(solution)/shard_map/rev | solution.py:69
  24.8 2.8 %reshape.99 = f32[32,1,8192,2]{2,0,3,1:T(8,128)} reshape(f32[32,32,256,2]{2,1,0,3:T(8,128)} %rev.3) | data formatting | bytes 4194304 | tf_op jit(solution)/shard_map/reshape
  27.6 8.2 %all-to-all-done = bf16[1024,8,32]{0,2,1:T(8,128)(2,1)S(1)} async-done(((bf16[1024,8,32]{0,2,1:T(8,128)(2,1)}), bf16[1024,8,32]{0,2,1:T(8,128)(2,1)S(1)}, u32[]{:S(2)}, u32[]{:S(2)}) %all-to-all-start) | async-done | bytes 524320 | tf_op jit(solution)/shard_map/all_to_all | solution.py:97
  35.9 0.2 fusion.14
  36.1 0.2 bitcast_dynamic-update-slice_fusion.1
  36.3 0.3 bitcast_dynamic-update-slice_fusion
  36.6 0.6 fusion.17
  37.2 0.6 convolution_add_fusion
  37.7 4.8 %reshape.109 = f32[1,95,8192,1]{2,0,3,1:T(1,128)} reshape(f32[95,32,256]{2,1,0:T(8,128)S(1)} %convolution_add_fusion) | data formatting | bytes 6225920 | tf_op jit(solution)/shard_map/reshape.1
  42.6 32.3 %convolution_reduce_fusion = f32[64,8192,2]{1,2,0:T(2,128)} fusion(f32[1,95,8192,1]{2,0,3,1:T(1,128)} %reshape.109, f32[32,1,8192,2]{2,0,3,1:T(8,128)} %reshape.99), kind=kOutput, calls=%fused_computation | convolution fusion | flops 201326592 | bytes 9404416 | tf_op jit(solution)/shard_map/convolution
  74.9 6.6 %reshape.100 = f32[64,32,256,2]{2,1,3,0:T(8,128)} reshape(f32[64,8192,2]{1,2,0:T(2,128)} %convolution_reduce_fusion) | data formatting | bytes 8388608 | tf_op jit(solution)/shard_map/reshape | solution.py:81
  81.6 2.5 %fusion.49 = (f32[64,32,256,1]{2,1,3,0:T(8,128)S(1)}, f32[64,32,256,1]{2,1,3,0:T(8,128)S(1)}) fusion(f32[64,32,256,2]{2,1,3,0:T(8,128)} %reshape.100), kind=kLoop, calls=%fused_computation.83 | loop fusion | bytes 8388608 | tf_op jit(solution)/shard_map/slice | solution.py:83
  84.1 1.2 %copy.38 = f32[64,32,256,1]{2,0,1,3:T(8,128)S(1)} copy(f32[64,32,256,1]{2,1,3,0:T(8,128)S(1)} %get-tuple-element.7) | data formatting | bytes 4194304
  85.3 1.2 %copy.39 = f32[64,32,256,1]{2,0,1,3:T(8,128)S(1)} copy(f32[64,32,256,1]{2,1,3,0:T(8,128)S(1)} %get-tuple-element.8) | data formatting | bytes 4194304
  86.6 0.3 slice_subtract_fusion
  86.9 1.0 fusion.8
  87.9 0.0 copy-start.1
  87.9 0.0 copy-start.2
  87.9 0.2 convert_element_type.80
  88.2 1.1 copy.25
  89.3 3.6 %all-to-all-start.2 = ((bf16[8,1024,32]{1,2,0:T(8,128)(2,1)}), bf16[8,1024,32]{1,2,0:T(8,128)(2,1)S(1)}, u32[]{:S(2)}, u32[]{:S(2)}) async-start(bf16[8,1024,32]{1,2,0:T(8,128)(2,1)} %copy.25), calls=%async_computation.2 | async-start | bytes 1048576 | tf_op jit(solution)/shard_map/all_to_all | solution.py:104
  92.9 0.0 copy-done.1
  92.9 0.2 copy.11
  93.1 14.2 %all-to-all-done.2 = bf16[8,1024,32]{1,2,0:T(8,128)(2,1)S(1)} async-done(((bf16[8,1024,32]{1,2,0:T(8,128)(2,1)}), bf16[8,1024,32]{1,2,0:T(8,128)(2,1)S(1)}, u32[]{:S(2)}, u32[]{:S(2)}) %all-to-all-start.2) | async-done | bytes 524320 | tf_op jit(solution)/shard_map/all_to_all | solution.py:104
  107.3 0.0 copy-done.2
  107.3 1.4 %multiply_reduce_fusion = f32[1024]{0:T(1024)S(1)} fusion(bf16[1024,256]{0,1:T(8,128)(2,1)} %multiply_convert_fusion, f32[256]{0:T(256)S(1)} %copy-done.2, bf16[1024,256]{0,1:T(8,128)(2,1)S(1)} %copy.11, bf16[8,1024,32]{1,2,0:T(8,128)(2,1)S(1)} %all-to-all-done.2), kind=kLoop, calls=%fused_computation.20 | loop fusion | flops 2096128 | bytes 1577984 | tf_op jit(solution)/shard_map/reduce_sum | solution.py:110
  108.7 5.7 %psum.7 = f32[1024]{0:T(1024)S(1)} all-reduce(f32[1024]{0:T(1024)S(1)} %multiply_reduce_fusion), channel_id=1, replica_groups=mesh['seq'=8,'mp'=4] {'mp'}, use_global_device_ids=true, to_apply=%region_1.2 | all-reduce | flops 1024 | bytes 8192 | tf_op jit(solution)/shard_map/psum | solution.py:111
  114.4 1.4 %divide_convert_fusion = bf16[1024,256]{0,1:T(8,128)(2,1)S(1)} fusion(f32[1024]{0:T(1024)S(1)} %add_sqrt_fusion, bf16[1024,256]{0,1:T(8,128)(2,1)} %multiply_convert_fusion, f32[256]{0:T(256)S(1)} %copy-done.2, bf16[1024,256]{0,1:T(8,128)(2,1)S(1)} %copy.11, bf16[8,1024,32]{1,2,0:T(8,128)(2,1)S(1)} %all-to-all-done.2), kind=kLoop, calls=%fused_computation.19 | loop fusion | flops 2097152 | bytes 2102272 | tf_op jit(solution)/shard_map/convert_element_type | solution.py:112
  115.8 1.0 copy.26
  (6 shorter events, 0.1 us)
Async XLA Ops:
  0.0 10.5 %copy-start = (bf16[1024,256]{1,0:T(8,128)(2,1)S(1)}, bf16[1024,256]{1,0:T(8,128)(2,1)}, u32[]{:S(2)}) copy-start(bf16[1024,256]{1,0:T(8,128)(2,1)} %param.6) | copy-start | bytes 1572868
  1.9 16.2 %all-to-all-start.1 = ((bf16[512,8,32]{0,2,1:T(8,128)(2,1)}), bf16[512,8,32]{0,2,1:T(8,128)(2,1)S(1)}, u32[]{:S(2)}, u32[]{:S(2)}) async-start(bf16[512,8,32]{0,2,1:T(8,128)(2,1)} %bitcast.5), calls=%async_computation.1 | async-start | bytes 524288 | tf_op jit(solution)/shard_map/all_to_all | solution.py:98
  18.1 17.8 %all-to-all-start = ((bf16[1024,8,32]{0,2,1:T(8,128)(2,1)}), bf16[1024,8,32]{0,2,1:T(8,128)(2,1)S(1)}, u32[]{:S(2)}, u32[]{:S(2)}) async-start(bf16[1024,8,32]{0,2,1:T(8,128)(2,1)} %bitcast.1), calls=%async_computation | async-start | bytes 1048576 | tf_op jit(solution)/shard_map/all_to_all | solution.py:97
  87.9 5.0 %copy-start.1 = (bf16[1024,256]{1,0:T(8,128)(2,1)S(1)}, bf16[1024,256]{1,0:T(8,128)(2,1)}, u32[]{:S(2)}) copy-start(bf16[1024,256]{1,0:T(8,128)(2,1)} %param.7) | copy-start | bytes 1572868
  87.9 19.4 %copy-start.2 = (f32[256]{0:T(256)S(1)}, f32[256]{0:T(256)}, u32[]{:S(2)}) copy-start(f32[256]{0:T(256)} %param.9) | copy-start | bytes 3076
  89.3 18.0 %all-to-all-start.2 = ((bf16[8,1024,32]{1,2,0:T(8,128)(2,1)}), bf16[8,1024,32]{1,2,0:T(8,128)(2,1)S(1)}, u32[]{:S(2)}, u32[]{:S(2)}) async-start(bf16[8,1024,32]{1,2,0:T(8,128)(2,1)} %copy.25), calls=%async_computation.2 | async-start | bytes 1048576 | tf_op jit(solution)/shard_map/all_to_all | solution.py:104
where the time goes:
time: 118 us; the launch traced here: 117 us
  matrix products  35.1 us (30%)
  waiting for transfers between devices  28 us (24%)
  local copies, waits for them, and re-layouts  27.9 us (24%)
  starting transfers between devices  14.5 us (12%)
  blocking collectives  5.67 us (5%)
  other arithmetic  5.42 us (5%)
    another operation x1, matrix products  32.3 us
    all_to_all x1, waiting for transfers between devices, local(): lax.all_to_all(shortened(channel_result), 'seq', split_axis=0, concat_axi...  14.2 us
    all_to_all x1, waiting for transfers between devices, local(): lax.all_to_all(gated, 'seq', split_axis=1, concat_axis=0, tiled=True)  8.22 us
    all_to_all x1, starting transfers between devices, local(): lax.all_to_all(filter_taps, 'seq', split_axis=1, concat_axis=0, tiled=True)  7.31 us
    reshape x1, local copies, waits for them, and re-layouts, convolve(): merged = merged.reshape(-1, channels, 2 * P_SIZE, 2)  6.65 us
    unnamed x14, local copies, waits for them, and re-layouts  6.38 us
    psum x1, blocking collectives, local(): totals = lax.psum(squares, 'mp')  5.67 us
    all_to_all x1, waiting for transfers between devices, local(): lax.all_to_all(filter_taps, 'seq', split_axis=1, concat_axis=0, tiled=True)  5.57 us
  transfers between devices with their start and end apart: 3, of which 3 were waited for; matrix products, arithmetic and copies ran while one was open for 8% of the time, Pallas kernels for 0%

commit v1 on v0

v1 whole, which is shorter than its diff:
```python
import functools

import jax
import jax.numpy as jnp
from jax import lax
from jax.experimental import pallas as pl
from jax.experimental.pallas import tpu as pltpu
from jax.sharding import PartitionSpec as P

LANES = 128
HALF = LANES // 2
WIDE = 2 * LANES
BF16 = jnp.bfloat16
F32 = jnp.float32
NT = (((1,), (1,)), ((), ()))


def vmem_call(body, out_shape, scratch=(), flops=0, name=None):
    return pl.pallas_call(
        body,
        out_shape=out_shape,
        scratch_shapes=list(scratch),
        cost_estimate=pl.CostEstimate(flops=flops, bytes_accessed=0, transcendentals=0),
        name=name,
    )


def unit_matrix(size):
    row = lax.broadcasted_iota(jnp.int32, (size, size), 0)
    column = lax.broadcasted_iota(jnp.int32, (size, size), 1)
    return jnp.where(row == column, 1.0, 0.0).astype(BF16)


def flip(matrix, unit):
    return lax.dot_general(unit, matrix, NT, preferred_element_type=F32).astype(BF16)


def prepare(gate_ref, value_ref, taps_ref, og_ref, gated_ref, taps_out_ref, og_out_ref):
    channels = gate_ref.shape[1]
    unit = unit_matrix(channels)
    step = min(WIDE, gate_ref.shape[0])
    for start in range(0, gate_ref.shape[0], step):
        rows = pl.ds(start, step)
        gated = (gate_ref[rows, :].astype(F32) * value_ref[rows, :].astype(F32)).astype(BF16)
        gated_ref[:, rows] = flip(gated, unit)
        og_out_ref[:, rows] = flip(og_ref[rows, :], unit)
    taps_out_ref[...] = flip(taps_ref[...], unit)


def conv_body(x_ref, h_ref, y_ref, xs, hs, xp, xr, lhs, rhs, s1, s2, ys):
    sources, channels, span = x_ref.shape
    per_source = span // LANES
    blocks = sources * per_source
    h_sources, _, h_span = h_ref.shape
    h_per = h_span // LANES
    h_blocks = h_sources * h_per
    pieces = lhs.shape[1] // LANES
    pad = xp.shape[0] - blocks
    for s in range(sources):
        for b in range(per_source):
            at = (s * per_source + b) * channels
            xs[pl.ds(at, channels), :] = x_ref[s, :, pl.ds(b * LANES, LANES)].astype(F32)
    for s in range(h_sources):
        for b in range(h_per):
            at = (s * h_per + b) * channels
            hs[pl.ds(at, channels), :] = h_ref[s, :, pl.ds(b * LANES, LANES)].astype(F32)
    xp[pl.ds(0, pad), :] = jnp.zeros((pad, LANES), F32)
    xr[pl.ds(0, pad), :] = jnp.zeros((pad, LANES), F32)
    s1[pl.ds(0, 8), :] = jnp.zeros((8, LANES), F32)
    s2[pl.ds(0, 8), :] = jnp.zeros((8, LANES), F32)
    rhs[pl.ds(h_blocks * HALF // 2, LANES), :] = jnp.zeros((LANES, WIDE), BF16)
    lane = lax.broadcasted_iota(jnp.int32, (HALF, LANES), 1)
    row = lax.broadcasted_iota(jnp.int32, (HALF, LANES), 0)
    ahead = lane >= row
    low = lax.broadcasted_iota(jnp.int32, (blocks, LANES), 1) < HALF

    def channel(c, carry):
        before = jnp.zeros((HALF, LANES), F32)
        for m in range(h_blocks + 1):
            if m < h_blocks:
                line = jnp.broadcast_to(hs[pl.ds(m * channels + c, 1), :], (HALF, LANES))
                now = pltpu.roll(line, 0, 1, stride=1, stride_axis=0)
            else:
                now = jnp.zeros((HALF, LANES), F32)
            tile = jnp.where(ahead, now, before).astype(BF16)
            rhs[pl.ds((m // 2) * HALF, HALF), pl.ds((m % 2) * LANES, LANES)] = tile
            before = now
        x = xs[pl.ds(c, blocks, stride=channels), :]
        xp[pl.ds(pad, blocks), :] = x
        xr[pl.ds(pad, blocks), :] = pltpu.roll(x, HALF, 1)
        for p in range(pieces):
            near = pl.ds(pad - 4 * p, blocks)
            far = pl.ds(pad - 4 * p - 2, blocks)
            at = pl.ds(p * LANES, LANES)
            lhs[pl.ds(0, blocks), at] = jnp.where(low, xp[near, :], xr[far, :]).astype(BF16)
            lhs[pl.ds(blocks, blocks), at] = jnp.where(low, xr[near, :], xp[far, :]).astype(BF16)
        z = jnp.dot(lhs[...], rhs[...], preferred_element_type=F32)
        first = pltpu.roll(z[blocks:, :LANES], HALF, 1)
        second = pltpu.roll(z[blocks:, LANES:], HALF, 1)
        s1[pl.ds(8, blocks), :] = z[:blocks, LANES:] + jnp.where(low, first, second)
        s2[pl.ds(8, blocks), :] = jnp.where(low, second, 0.0)
        y = z[:blocks, :LANES] + jnp.where(low, 0.0, first)
        y = y + s1[pl.ds(7, blocks), :] + s2[pl.ds(6, blocks), :]
        ys[pl.ds(c, blocks, stride=channels), :] = y
        return carry

    lax.fori_loop(0, channels, channel, 0)
    for s in range(sources):
        for b in range(per_source):
            at = (s * per_source + b) * channels
            y_ref[s, :, pl.ds(b * LANES, LANES)] = ys[pl.ds(at, channels), :].astype(BF16)


def convolve(x, h):
    sources, channels, span = x.shape
    if h.shape[2] % LANES:
        h = jnp.moveaxis(h, 0, 1).reshape(1, channels, -1)
    blocks = sources * span // LANES
    taps = h.shape[0] * h.shape[2]
    h_blocks = taps // LANES
    deep = h_blocks * HALF // 2 * 1 + LANES
    pieces = deep // LANES
    pad = -(-(4 * pieces) // 8) * 8
    scratch = [
        pltpu.VMEM((blocks * channels, LANES), F32),
        pltpu.VMEM((h_blocks * channels, LANES), F32),
        pltpu.VMEM((pad + blocks, LANES), F32),
        pltpu.VMEM((pad + blocks, LANES), F32),
        pltpu.VMEM((2 * blocks, deep), BF16),
        pltpu.VMEM((deep, WIDE), BF16),
        pltpu.VMEM((8 + blocks, LANES), F32),
        pltpu.VMEM((8 + blocks, LANES), F32),
        pltpu.VMEM((blocks * channels, LANES), F32),
    ]
    return vmem_call(
        conv_body,
        jax.ShapeDtypeStruct(x.shape, BF16),
        scratch,
        flops=2 * channels * 2 * blocks * deep * WIDE,
        name="conv",
    )(x, h)


def mix(conv_ref, gated_ref, og_ref, skip_ref, mixed_ref, power_ref):
    mixed = og_ref[...].astype(F32) * (
        conv_ref[...].astype(F32) + skip_ref[...] * gated_ref[...].astype(F32)
    )
    mixed_ref[...] = mixed
    power_ref[...] = jnp.sum(mixed * mixed, axis=0, keepdims=True)


def finish(total, mixed_ref, power_ref, out_ref):
    scale = 1.0 / jnp.sqrt(power_ref[...] / total + 1e-05)
    step = min(WIDE, out_ref.shape[0])
    unit = unit_matrix(step)
    for start in range(0, out_ref.shape[0], step):
        rows = pl.ds(start, step)
        out_ref[rows, :] = flip((mixed_ref[:, rows] * scale[:, start : start + step]).astype(BF16), unit)


def spread_sum(value, axis, size):
    total = value
    for d in range(1, size):
        total = total + lax.ppermute(value, axis, [(j, (j + d) % size) for j in range(size)])
    return total


def local(n_seq, n_mp, gate_in, value_in, out_gate, filter_taps, skip_gain):
    tokens, channels = gate_in.shape
    taps = filter_taps.shape[0]
    share = channels // n_seq
    gated, taps_t, og = vmem_call(
        prepare,
        (
            jax.ShapeDtypeStruct((channels, tokens), BF16),
            jax.ShapeDtypeStruct((channels, taps), BF16),
            jax.ShapeDtypeStruct((channels, tokens), BF16),
        ),
        name="prepare",
        flops=4 * channels * channels * tokens,
    )(gate_in, value_in, filter_taps, out_gate)
    swap = functools.partial(lax.all_to_all, axis_name="seq", split_axis=0, concat_axis=0, tiled=True)
    h = swap(taps_t.reshape(n_seq, share, taps))
    x = swap(gated.reshape(n_seq, share, tokens))
    y = swap(convolve(x, h)).reshape(channels, tokens)
    mixed, power = vmem_call(
        mix,
        (
            jax.ShapeDtypeStruct((channels, tokens), F32),
            jax.ShapeDtypeStruct((1, tokens), F32),
        ),
        name="mix",
        flops=8 * channels * tokens,
    )(y, gated, og, skip_gain.reshape(channels, 1))
    power = spread_sum(power, "mp", n_mp)
    return vmem_call(
        functools.partial(finish, channels * n_mp),
        jax.ShapeDtypeStruct((tokens, channels), BF16),
        name="finish",
        flops=4 * channels * tokens * WIDE,
    )(mixed, power)


def solution(mesh):
    return jax.shard_map(
        functools.partial(local, mesh.shape["seq"], mesh.shape["mp"]),
        mesh=mesh,
        in_specs=(P("seq", "mp"), P("seq", "mp"), P("seq", "mp"), P("seq", "mp"), P("mp")),
        out_specs=P("seq", "mp"),
        check_vma=False,
    )
```

time: 118 us -> 87.7 us (0.74)
  matrix products: 35.1 us -> 0 us
  Pallas kernels: 0 us -> 28.6 us
  blocking collectives: 5.67 us -> 34.1 us
  local copies, waits for them, and re-layouts: 27.9 us -> 2.26 us
  waiting for transfers between devices: 28 us -> 15.6 us
  starting transfers between devices: 14.5 us -> 5.36 us
  other arithmetic: 5.42 us -> 1.27 us
    all_to_all x0 -> x2, blocking collectives: none -> 34.1 us  [the longest x1 17.6 us: local(): x = swap(gated.reshape(n_seq, share, tokens))]
    another operation x1 -> x0, matrix products: 32.3 us -> none
    pallas_call x0 -> x4, Pallas kernels: none -> 28.6 us  [the longest x1 20.6 us: convolve(): vmem_call(conv_body, jax.ShapeDtypeStruct(x.shape, BF16), scratch, flops=...]
    all_to_all x3 -> x1, waiting for transfers between devices: 28 us -> 12.6 us  [local(): y = swap(convolve(x, h)).reshape(channels, tokens)]
    all_to_all x3 -> x1, starting transfers between devices: 14.5 us -> 3.64 us  [local(): y = swap(convolve(x, h)).reshape(channels, tokens)]
    reshape x4 -> x1, local copies, waits for them, and re-layouts: 9.71 us -> 0.8 us  [local(): skip_gain.reshape(channels, 1)]
    psum x1 -> x0, blocking collectives: 5.67 us -> none  [local(): totals = lax.psum(squares, 'mp')]
    unnamed x14 -> x6, local copies, waits for them, and re-layouts: 6.38 us -> 1.47 us
  transfers between devices with their start and end apart: 3 -> 4, of which waited for: 3 -> 3; matrix products, arithmetic and copies ran while one was open for 8% -> 1% of each run, Pallas kernels for 0% -> 0%
where the time goes in v1:
time: 87.7 us; the launch traced here: 87.2 us
  blocking collectives  34.1 us (39%)
  Pallas kernels  28.6 us (33%)
  waiting for transfers between devices  15.6 us (18%)
  starting transfers between devices  5.36 us (6%)
  local copies, waits for them, and re-layouts  2.26 us (3%)
  other arithmetic  1.27 us (1%)
    pallas_call x1, Pallas kernels, convolve(): vmem_call(conv_body, jax.ShapeDtypeStruct(x.shape, BF16), scratch, flops=...  20.6 us
    all_to_all x1, blocking collectives, local(): x = swap(gated.reshape(n_seq, share, tokens))  17.6 us
    all_to_all x1, blocking collectives, local(): h = swap(taps_t.reshape(n_seq, share, taps))  16.5 us
    all_to_all x1, waiting for transfers between devices, local(): y = swap(convolve(x, h)).reshape(channels, tokens)  12.6 us
    all_to_all x1, starting transfers between devices, local(): y = swap(convolve(x, h)).reshape(channels, tokens)  3.64 us
    ppermute x3, waiting for transfers between devices, spread_sum(): lax.ppermute(value, axis, [(j, (j + d) % size) for j in range(size)])  3.01 us
    pallas_call x1, Pallas kernels, local(): vmem_call(prepare, (jax.ShapeDtypeStruct((channels, tokens), BF16), jax.S...  3 us
    pallas_call x1, Pallas kernels, local(): vmem_call(mix, (jax.ShapeDtypeStruct((channels, tokens), F32), jax.ShapeD...  2.67 us
  transfers between devices with their start and end apart: 4, of which 3 were waited for; matrix products, arithmetic and copies ran while one was open for 1% of the time, Pallas kernels for 0%

profile of v1, /device:TPU:0, one launch (start us, length us, event | category | flops | bytes accessed | tf_op | source)
XLA Modules:
  0.0 87.2 jit_solution(13417429346650704012)
XLA Ops:
  0.0 3.0 %prepare.1 = (bf16[256,1024]{1,0:T(8,128)(2,1)}, bf16[256,512]{1,0:T(8,128)(2,1)}, bf16[256,1024]{1,0:T(8,128)(2,1)}) custom-call(bf16[1024,256]{1,0:T(8,128)(2,1)} %gate_ref.1, bf16[1024,256]{1,0:T(8,128)(2,1)} %value_ref.1, bf16[512,256]{1,0:T(8,128)(2,1)} %taps_ref.1, bf16[1024,256]{1,0:T(8,128)(2,1)} %og_ref.1), custom_call_target="tpu_custom_call" | custom-call | flops 268435456 | tf_op jit(solution)/shard_map/prepare/pallas_call | solution.py:172
  3.0 0.0 copy-start
  3.0 16.5 %all_to_all.15.h_ref = bf16[8,32,512]{2,1,0:T(8,128)(2,1)} all-to-all(bf16[8,32,512]{2,1,0:T(8,128)(2,1)} %bitcast.6), channel_id=1, replica_groups=mesh['seq'=8,'mp'=4] {'seq'}, dimensions={0} | all-to-all | bytes 524288 | tf_op jit(solution)/shard_map/all_to_all | solution.py:183
  19.5 0.0 copy-done
  19.5 17.6 %all_to_all.16.x_ref = bf16[8,32,1024]{2,1,0:T(8,128)(2,1)} all-to-all(bf16[8,32,1024]{2,1,0:T(8,128)(2,1)S(1)} %bitcast.4), channel_id=1, replica_groups=mesh['seq'=8,'mp'=4] {'seq'}, dimensions={0} | all-to-all | bytes 1048576 | tf_op jit(solution)/shard_map/all_to_all | solution.py:184
  37.1 20.6 %conv.1 = bf16[8,32,1024]{2,1,0:T(8,128)(2,1)} custom-call(bf16[8,32,1024]{2,1,0:T(8,128)(2,1)} %all_to_all.16.x_ref, bf16[8,32,512]{2,1,0:T(8,128)(2,1)} %all_to_all.15.h_ref), custom_call_target="tpu_custom_call" | custom-call | flops 2415919104 | tf_op jit(solution)/shard_map/conv/pallas_call | solution.py:135
  57.7 3.6 %all-to-all-start.2 = ((bf16[8,32,1024]{2,1,0:T(8,128)(2,1)}), bf16[8,32,1024]{2,1,0:T(8,128)(2,1)S(1)}, u32[]{:S(2)}, u32[]{:S(2)}) async-start(bf16[8,32,1024]{2,1,0:T(8,128)(2,1)} %conv.1), calls=%async_computation.2 | async-start | bytes 1048576 | tf_op jit(solution)/shard_map/all_to_all | solution.py:185
  61.3 0.0 copy-start.2
  61.3 0.7 copy-done.2
  62.0 0.8 copy.6.skip_ref
  62.8 12.6 %all-to-all-done.2 = bf16[8,32,1024]{2,1,0:T(8,128)(2,1)S(1)} async-done(((bf16[8,32,1024]{2,1,0:T(8,128)(2,1)}), bf16[8,32,1024]{2,1,0:T(8,128)(2,1)S(1)}, u32[]{:S(2)}, u32[]{:S(2)}) %all-to-all-start.2) | async-done | bytes 524320 | tf_op jit(solution)/shard_map/all_to_all | solution.py:185
  75.4 0.0 copy-start.1
  75.4 0.8 copy-done.1
  76.2 2.7 %mix.1 = (f32[256,1024]{1,0:T(8,128)}, f32[1,1024]{1,0:T(1,128)}) custom-call(bf16[256,1024]{1,0:T(8,128)(2,1)} %bitcast.5, bf16[256,1024]{1,0:T(8,128)(2,1)} %get-tuple-element.10.gated_ref, bf16[256,1024]{1,0:T(8,128)(2,1)} %get-tuple-element.12.og_ref, f32[256,1]{1,0:T(8,128)} %copy.6.skip_ref), custom_call_target="tpu_custom_call" | custom-call | flops 2097152 | tf_op jit(solution)/shard_map/mix/pallas_call | solution.py:186
  78.9 0.0 collective-permute-start.2
  78.9 1.5 %collective-permute-start.1 = (f32[1,1024]{1,0:T(1,128)}, f32[1,1024]{1,0:T(1,128)S(1)}, u32[]{:S(2)}, u32[]{:S(2)}) collective-permute-start(f32[1,1024]{1,0:T(1,128)} %get-tuple-element.14), channel_id=1, source_target_pairs={{0,2},{1,3},{2,0},{3,1},{4,6},{5,7},{6,4},{7,5},{8,10},{9,11},{10,... | collective-permute-start | bytes 12296 | tf_op jit(solution)/shard_map/ppermute | solution.py:164
  80.3 0.2 collective-permute-start
  80.6 0.0 collective-permute-done.2
  80.6 2.1 %collective-permute-done.1 = f32[1,1024]{1,0:T(1,128)S(1)} collective-permute-done((f32[1,1024]{1,0:T(1,128)}, f32[1,1024]{1,0:T(1,128)S(1)}, u32[]{:S(2)}, u32[]{:S(2)}) %collective-permute-start.1) | collective-permute-done | bytes 4128 | tf_op jit(solution)/shard_map/ppermute | solution.py:164
  82.7 0.9 %collective-permute-done = f32[1,1024]{1,0:T(1,128)S(1)} collective-permute-done((f32[1,1024]{1,0:T(1,128)}, f32[1,1024]{1,0:T(1,128)S(1)}, u32[]{:S(2)}, u32[]{:S(2)}) %collective-permute-start) | collective-permute-done | bytes 4128 | tf_op jit(solution)/shard_map/ppermute | solution.py:164
  83.6 1.3 %add_add_fusion.power_ref = f32[1,1024]{1,0:T(1,128)} fusion(f32[1,1024]{1,0:T(1,128)S(1)} %collective-permute-done.2, f32[1,1024]{1,0:T(1,128)S(1)} %collective-permute-done.1, f32[1,1024]{1,0:T(1,128)} %get-tuple-element.14, f32[1,1024]{1,0:T(1,128)S(1)} %collective-permute-done), kind=kLoop, calls=%fused_computation | loop fusion | flops 3072 | bytes 20480 | tf_op jit(solution)/shard_map/add | solution.py:164
  84.9 2.4 %finish.1 = bf16[1024,256]{1,0:T(8,128)(2,1)} custom-call(f32[256,1024]{1,0:T(8,128)} %get-tuple-element.13.mixed_ref, f32[1,1024]{1,0:T(1,128)} %add_add_fusion.power_ref), custom_call_target="tpu_custom_call" | custom-call | flops 268435456 | tf_op jit(solution)/shard_map/finish/pallas_call | solution.py:196
Async XLA Ops:
  3.0 16.5 %copy-start = (bf16[256,1024]{1,0:T(8,128)(2,1)S(1)}, bf16[256,1024]{1,0:T(8,128)(2,1)}, u32[]{:S(2)}) copy-start(bf16[256,1024]{1,0:T(8,128)(2,1)} %get-tuple-element.10.gated_ref) | copy-start | bytes 1572868
  57.7 17.7 %all-to-all-start.2 = ((bf16[8,32,1024]{2,1,0:T(8,128)(2,1)}), bf16[8,32,1024]{2,1,0:T(8,128)(2,1)S(1)}, u32[]{:S(2)}, u32[]{:S(2)}) async-start(bf16[8,32,1024]{2,1,0:T(8,128)(2,1)} %conv.1), calls=%async_computation.2 | async-start | bytes 1048576 | tf_op jit(solution)/shard_map/all_to_all | solution.py:185
  61.3 0.7 copy-start.2
  75.4 0.8 copy-start.1
  78.9 1.7 %collective-permute-start.2 = (f32[1,1024]{1,0:T(1,128)}, f32[1,1024]{1,0:T(1,128)S(1)}, u32[]{:S(2)}, u32[]{:S(2)}) collective-permute-start(f32[1,1024]{1,0:T(1,128)} %get-tuple-element.14), channel_id=1, source_target_pairs={{0,3},{1,0},{2,1},{3,2},{4,7},{5,4},{6,5},{7,6},{8,11},{9,8},{10,9... | collective-permute-start | bytes 12296 | tf_op jit(solution)/shard_map/ppermute | solution.py:164
  78.9 3.8 %collective-permute-start.1 = (f32[1,1024]{1,0:T(1,128)}, f32[1,1024]{1,0:T(1,128)S(1)}, u32[]{:S(2)}, u32[]{:S(2)}) collective-permute-start(f32[1,1024]{1,0:T(1,128)} %get-tuple-element.14), channel_id=1, source_target_pairs={{0,2},{1,3},{2,0},{3,1},{4,6},{5,7},{6,4},{7,5},{8,10},{9,11},{10,... | collective-permute-start | bytes 12296 | tf_op jit(solution)/shard_map/ppermute | solution.py:164
  80.3 3.2 %collective-permute-start = (f32[1,1024]{1,0:T(1,128)}, f32[1,1024]{1,0:T(1,128)S(1)}, u32[]{:S(2)}, u32[]{:S(2)}) collective-permute-start(f32[1,1024]{1,0:T(1,128)} %get-tuple-element.14), channel_id=1, source_target_pairs={{0,1},{1,2},{2,3},{3,0},{4,5},{5,6},{6,7},{7,4},{8,9},{9,10},{10,1... | collective-permute-start | bytes 12296 | tf_op jit(solution)/shard_map/ppermute | solution.py:164

commit v2 on v1

v2 whole, which is shorter than its diff:
```python
import functools

import jax
import jax.numpy as jnp
from jax import lax
from jax.experimental import pallas as pl
from jax.experimental.pallas import tpu as pltpu
from jax.sharding import PartitionSpec as P

LANES = 128
HALF = LANES // 2
WIDE = 2 * LANES
CHUNKS = 1
BF16 = jnp.bfloat16
F32 = jnp.float32
NT = (((1,), (1,)), ((), ()))


def vmem_call(body, out_shape, scratch=(), flops=0, name=None, limit=6, inputs=1):
    spec = pl.BlockSpec(memory_space=pltpu.VMEM)
    return pl.pallas_call(
        body,
        out_shape=out_shape,
        in_specs=[spec] * inputs,
        out_specs=[spec] * len(out_shape) if isinstance(out_shape, (list, tuple)) else spec,
        scratch_shapes=list(scratch),
        compiler_params=pltpu.CompilerParams(vmem_limit_bytes=limit << 20),
        cost_estimate=pl.CostEstimate(flops=flops, bytes_accessed=0, transcendentals=0),
        name=name,
    )


def unit_matrix(size):
    row = lax.broadcasted_iota(jnp.int32, (size, size), 0)
    column = lax.broadcasted_iota(jnp.int32, (size, size), 1)
    return jnp.where(row == column, 1.0, 0.0).astype(BF16)


def flip(matrix, unit):
    return lax.dot_general(unit, matrix, NT, preferred_element_type=F32).astype(BF16)


def deal(flipped, refs, span):
    owners, part, _ = refs[0].shape
    for owner in range(owners):
        for k, ref in enumerate(refs):
            at = (owner * len(refs) + k) * part
            ref[owner, :, span] = flipped[at : at + part, :]


def flip_in(gate_ref, value_ref, taps_ref, *out_refs):
    unit = unit_matrix(gate_ref.shape[1])
    tokens = gate_ref.shape[0]
    step = min(WIDE, tokens)

    def some(i, carry):
        rows = pl.ds(pl.multiple_of(i * step, step), step)
        gated = (gate_ref[rows, :].astype(F32) * value_ref[rows, :].astype(F32)).astype(BF16)
        deal(flip(gated, unit), out_refs, rows)
        return carry

    lax.fori_loop(0, tokens // step, some, 0)
    deal(flip(taps_ref[...], unit), out_refs, pl.ds(tokens, taps_ref.shape[0]))


def flip_out_gate(og_ref, skip_ref, column_ref, *out_refs):
    unit = unit_matrix(og_ref.shape[1])
    step = min(WIDE, og_ref.shape[0])

    def some(i, carry):
        rows = pl.ds(pl.multiple_of(i * step, step), step)
        deal(flip(og_ref[rows, :], unit), out_refs, rows)
        return carry

    lax.fori_loop(0, og_ref.shape[0] // step, some, 0)
    column_ref[...] = jnp.broadcast_to(skip_ref[...], (LANES, skip_ref.shape[1])).T


UNROLL = 2
PACK = 16

def conv_body(*refs):
    x_ref, h_ref = refs[0], refs[-6]
    y_ref, vs, hs, zs0, zs1 = refs[-5:]
    sources, channels, span = y_ref.shape
    per_source = span // LANES
    blocks = sources * per_source
    h_sources = h_ref.shape[0]
    h_from = span if h_ref is x_ref else 0
    h_per = (h_ref.shape[2] - h_from) // LANES
    h_blocks = h_sources * h_per
    rows = 2 * blocks
    pitch = channels + 8
    low = lax.broadcasted_iota(jnp.int32, (channels, LANES), 1) < HALF
    zero = jnp.zeros((channels, LANES), F32)

    def place(s, b, j):
        at = (8 * (per_source * s // 4 + b // 4) + 4 * j + b % 4) * pitch
        return pl.ds(at if pitch % 8 else pl.multiple_of(at, 8), channels)

    def spread(s, carry):
        older, old = carry
        for b in range(per_source):
            x = x_ref[s, :, pl.ds(b * LANES, LANES)].astype(F32)
            turned = pltpu.roll(x, HALF, 1)
            vs[place(s, b, 0), :] = jnp.where(low, x, older[1])
            vs[place(s, b, 1), :] = jnp.where(low, turned, older[0])
            older, old = old, (x, turned)
        return older, old

    lax.fori_loop(0, sources, spread, ((zero, zero), (zero, zero)))

    def spread_taps(s, carry):
        for b in range(h_per):
            at = (s * h_per + b) * pitch
            at = at if pitch % 8 else pl.multiple_of(at, 8)
            hs[pl.ds(at, channels), :] = h_ref[s, :, pl.ds(h_from + b * LANES, LANES)].astype(F32)
        return carry

    lax.fori_loop(0, h_sources, spread_taps, 0)

    lane = lax.broadcasted_iota(jnp.int32, (PACK, LANES), 1)
    row = lax.broadcasted_iota(jnp.int32, (PACK, LANES), 0)
    ahead = lane >= row
    lane16 = lane.astype(F32).astype(BF16)

    def channel(c):
        v = vs[pl.ds(c, rows, stride=pitch), :]
        even = v.astype(BF16)
        odd = jnp.concatenate([jnp.zeros((8, LANES), F32), v[:-8]], axis=0).astype(BF16)
        before = jnp.zeros((PACK, LANES), F32)
        turns = [jnp.zeros((PACK, LANES), BF16)] * (HALF // PACK)
        tiles = []
        z = None
        for m in range(h_blocks + 1):
            if m < h_blocks:
                line = jnp.broadcast_to(hs[pl.ds(m * pitch + c, 1), :], (PACK, LANES))
                now = pltpu.roll(line, 0, 1, stride=1, stride_axis=0)
            else:
                now = jnp.zeros((PACK, LANES), F32)
            base = jnp.where(ahead, now, before).astype(BF16)
            before = now
            group = [base]
            for q in range(1, HALF // PACK):
                turned = pltpu.roll(base, PACK * q, 1)
                group.append(jnp.where(lane16 >= PACK * q, turned, turns[q]))
                turns[q] = turned
            tiles.append(jnp.concatenate(group, axis=0))
            if m % 8 == 7 or m == h_blocks:
                k = m // 8
                top = PACK * k
                left = rows - top
                if m < h_blocks:
                    weight = jnp.concatenate(
                        [jnp.concatenate(tiles[i : i + 2], axis=1) for i in range(0, 8, 2)], axis=0
                    )
                    data = jnp.concatenate([even[:left], odd[:left]], axis=1)
                else:
                    weight = jnp.concatenate([tiles[0], jnp.zeros((HALF, LANES), BF16)], axis=0)
                    weight = jnp.concatenate([weight, jnp.zeros((LANES, LANES), BF16)], axis=1)
                    data = even[:left]
                part = jnp.dot(data, weight, preferred_element_type=F32)
                z = part if z is None else jnp.concatenate([z[:top], z[top:] + part], axis=0)
                tiles = []
        zs0[pl.ds(c, rows, stride=pitch), :] = z[:, :LANES]
        zs1[pl.ds(c, rows, stride=pitch), :] = z[:, LANES:]

    def group(g, carry):
        for i in range(UNROLL):
            channel(g * UNROLL + i)
        return carry

    lax.fori_loop(0, channels // UNROLL, group, 0)

    def gather(s, carry):
        late1, late2, late22 = carry
        for b in range(per_source):
            first = pltpu.roll(zs0[place(s, b, 1), :], HALF, 1)
            second = pltpu.roll(zs1[place(s, b, 1), :], HALF, 1)
            y = zs0[place(s, b, 0), :] + jnp.where(low, 0.0, first) + late1 + late22
            late1 = zs1[place(s, b, 0), :] + jnp.where(low, first, second)
            late22, late2 = late2, jnp.where(low, second, 0.0)
            y_ref[s, :, pl.ds(b * LANES, LANES)] = y.astype(BF16)
        return late1, late2, late22

    lax.fori_loop(0, sources, gather, (zero, zero, zero))


def convolve(data, span):
    sources, channels, both = data.shape
    taps = sources * (both - span)
    inputs = [data]
    if (both - span) % LANES:
        inputs.append(jnp.moveaxis(data[:, :, span:], 0, 1).reshape(1, channels, taps))
    blocks = sources * span // LANES
    scratch = [
        pltpu.VMEM((2 * blocks * (channels + 8), LANES), F32),
        pltpu.VMEM((taps // LANES * (channels + 8), LANES), F32),
        pltpu.VMEM((2 * blocks * (channels + 8), LANES), F32),
        pltpu.VMEM((2 * blocks * (channels + 8), LANES), F32),
    ]
    return vmem_call(
        conv_body,
        jax.ShapeDtypeStruct((sources, channels, span), BF16),
        scratch,
        flops=4 * channels * blocks * (taps // 4 + HALF) * WIDE,
        name="conv",
        limit=28,
        inputs=len(inputs),
    )(*inputs)


def mix(k, chunks, has_before, y_ref, gated_ref, og_ref, column_ref, *refs):
    mixed_ref, power_ref = refs[-2:]
    owners, part, tokens = y_ref.shape
    power_ref[...] = refs[0][...] if has_before else jnp.zeros((8, tokens), F32)

    def some(owner, carry):
        at = (owner * chunks + k) * part
        skip = column_ref[pl.ds(at if part % 8 else pl.multiple_of(at, 8), part), :1]
        mixed = og_ref[owner].astype(F32) * (
            y_ref[owner].astype(F32) + skip * gated_ref[owner, :, :tokens].astype(F32)
        )
        mixed_ref[owner] = mixed
        square = mixed * mixed
        if part % 8:
            power_ref[pl.ds(0, 1), :] += jnp.sum(square, axis=0, keepdims=True)
        else:
            power_ref[...] += jnp.sum(square.reshape(part // 8, 8, tokens), axis=0)
        return carry

    lax.fori_loop(0, owners, some, 0)
    power_ref[...] = jnp.broadcast_to(jnp.sum(power_ref[...], axis=0, keepdims=True), (8, tokens))


def finish(total, peers, *refs):
    powers, mixed, out_ref = refs[:peers], refs[peers:-1], refs[-1]
    step = min(WIDE, out_ref.shape[0])
    unit = unit_matrix(step)
    owners = mixed[0].shape[0]

    def some(i, carry):
        rows = pl.ds(pl.multiple_of(i * step, step), step)
        power = powers[0][:1, rows]
        for other in powers[1:]:
            power = power + other[:1, rows]
        scale = 1.0 / jnp.sqrt(power / total + 1e-05)
        pieces = [
            (ref[owner, :, rows] * scale).astype(BF16) for owner in range(owners) for ref in mixed
        ]
        out_ref[rows, :] = flip(jnp.concatenate(pieces, axis=0), unit)
        return carry

    lax.fori_loop(0, out_ref.shape[0] // step, some, 0)


def local(n_seq, n_mp, gate_in, value_in, out_gate, filter_taps, skip_gain):
    tokens, channels = gate_in.shape
    taps = filter_taps.shape[0]
    share = channels // n_seq
    chunks = CHUNKS if share % (16 * CHUNKS) == 0 else 1
    part = share // chunks
    swap = functools.partial(lax.all_to_all, axis_name="seq", split_axis=0, concat_axis=0, tiled=True)
    dealt = [jax.ShapeDtypeStruct((n_seq, part, tokens), BF16)] * chunks
    dealt_both = [jax.ShapeDtypeStruct((n_seq, part, tokens + taps), BF16)] * chunks
    column = jax.ShapeDtypeStruct((channels, LANES), F32)
    flat = [jax.ShapeDtypeStruct((n_seq, part, tokens), F32), jax.ShapeDtypeStruct((8, tokens), F32)]
    product = 2 * channels * channels
    both = vmem_call(
        flip_in, dealt_both, name="flip_in", flops=product * (tokens + taps), inputs=3
    )(gate_in, value_in, filter_taps)
    moved = [swap(piece) for piece in both]
    skip, *og = vmem_call(
        flip_out_gate, [column] + dealt, name="flip_out_gate", flops=product * tokens, inputs=2
    )(out_gate, skip_gain.reshape(1, channels))
    y = [swap(convolve(piece, tokens)) for piece in moved]
    mixed, power = [], None
    for k in range(chunks):
        before = [] if power is None else [power]
        piece, power = vmem_call(
            functools.partial(mix, k, chunks, bool(before)),
            flat,
            name="mix",
            flops=8 * channels * tokens,
            inputs=4 + len(before),
        )(y[k], both[k], og[k], skip, *before)
        mixed.append(piece)
    powers = [power] + [
        lax.ppermute(power[:1], "mp", [(j, (j + d) % n_mp) for j in range(n_mp)])
        for d in range(1, n_mp)
    ]
    return vmem_call(
        functools.partial(finish, channels * n_mp, n_mp),
        jax.ShapeDtypeStruct((tokens, channels), BF16),
        name="finish",
        flops=2 * channels * tokens * WIDE,
        inputs=n_mp + chunks,
    )(*powers, *mixed)


def solution(mesh):
    return jax.shard_map(
        functools.partial(local, mesh.shape["seq"], mesh.shape["mp"]),
        mesh=mesh,
        in_specs=(P("seq", "mp"), P("seq", "mp"), P("seq", "mp"), P("seq", "mp"), P("mp")),
        out_specs=P("seq", "mp"),
        check_vma=False,
    )
```

time: 87.7 us -> 68.7 us (0.78)
  Pallas kernels: 28.6 us -> 16.5 us
  blocking collectives: 34.1 us -> 27.3 us
  local copies, waits for them, and re-layouts: 2.26 us -> 3.71 us
  other arithmetic: 1.27 us -> 0 us
    pallas_call x4 -> x5, Pallas kernels: 28.6 us -> 16.5 us  [the longest x1 11.7 us: convolve(): vmem_call(conv_body, jax.ShapeDtypeStruct((sources, channels, span), BF16...]
    all_to_all x2 -> x1, blocking collectives: 34.1 us -> 27.3 us  [local(): moved = [swap(piece) for piece in both]]
    unnamed x6 -> x10, local copies, waits for them, and re-layouts: 1.47 us -> 3.7 us
    add x1 -> x0, other arithmetic: 1.27 us -> none  [spread_sum(): total + lax.ppermute(value, axis, [(j, (j + d) % size) for j in range(siz...]
  transfers between devices with their start and end apart: 4 -> 4, of which waited for: 3 -> 3; matrix products, arithmetic and copies ran while one was open for 1% -> 0% of each run, Pallas kernels for 0% -> 1%
where the time goes in v2:
time: 68.7 us; the launch traced here: 68.4 us
  blocking collectives  27.3 us (40%)
  Pallas kernels  16.5 us (24%)
  waiting for transfers between devices  15.4 us (22%)
  starting transfers between devices  5.49 us (8%)
  local copies, waits for them, and re-layouts  3.71 us (5%)
    all_to_all x1, blocking collectives, local(): moved = [swap(piece) for piece in both]  27.3 us
    all_to_all x1, waiting for transfers between devices, local(): y = [swap(convolve(piece, tokens)) for piece in moved]  12.5 us
    pallas_call x1, Pallas kernels, convolve(): vmem_call(conv_body, jax.ShapeDtypeStruct((sources, channels, span), BF16...  11.7 us
    all_to_all x1, starting transfers between devices, local(): y = [swap(convolve(piece, tokens)) for piece in moved]  3.72 us
    unnamed x10, local copies, waits for them, and re-layouts  3.7 us
    ppermute x3, waiting for transfers between devices, local(): lax.ppermute(power[:1], 'mp', [(j, (j + d) % n_mp) for j in range(n_mp)])  2.88 us
    pallas_call x1, Pallas kernels, local(): vmem_call(functools.partial(finish, channels * n_mp, n_mp), jax.ShapeDtyp...  1.8 us
    ppermute x3, starting transfers between devices, local(): lax.ppermute(power[:1], 'mp', [(j, (j + d) % n_mp) for j in range(n_mp)])  1.76 us
  transfers between devices with their start and end apart: 4, of which 3 were waited for; matrix products, arithmetic and copies ran while one was open for 0% of the time, Pallas kernels for 1%

profile of v2, /device:TPU:0, one launch (start us, length us, event | category | flops | bytes accessed | tf_op | source)
XLA Modules:
  0.0 68.4 jit_solution(7767226776073676950)
XLA Ops:
  0.0 0.0 copy-start.1
  0.0 1.0 %copy-done.1 = bf16[1024,256]{1,0:T(8,128)(2,1)S(1)} copy-done((bf16[1024,256]{1,0:T(8,128)(2,1)S(1)}, bf16[1024,256]{1,0:T(8,128)(2,1)}, u32[]{:S(2)}) %copy-start.1) | copy-done | bytes 524312
  1.0 0.0 copy-start.2
  1.0 1.0 %copy-done.2 = bf16[1024,256]{1,0:T(8,128)(2,1)S(1)} copy-done((bf16[1024,256]{1,0:T(8,128)(2,1)S(1)}, bf16[1024,256]{1,0:T(8,128)(2,1)}, u32[]{:S(2)}) %copy-start.2) | copy-done | bytes 524312
  2.1 0.0 copy-start.3
  2.1 0.9 %copy-done.3 = bf16[512,256]{1,0:T(8,128)(2,1)S(1)} copy-done((bf16[512,256]{1,0:T(8,128)(2,1)S(1)}, bf16[512,256]{1,0:T(8,128)(2,1)}, u32[]{:S(2)}) %copy-start.3) | copy-done | bytes 262168
  3.0 1.2 %flip_in.1.gated_ref = bf16[8,32,1536]{2,1,0:T(8,128)(2,1)S(1)} custom-call(bf16[1024,256]{1,0:T(8,128)(2,1)S(1)} %copy-done.1, bf16[1024,256]{1,0:T(8,128)(2,1)S(1)} %copy-done.2, bf16[512,256]{1,0:T(8,128)(2,1)S(1)} %copy-done.3), custom_call_target="tpu_custom_call" | custom-call | flops 201326592 | tf_op jit(solution)/shard_map/flip_in/pallas_call | solution.py:269
  4.2 27.3 %all_to_all.10.refs_0_ = bf16[8,32,1536]{2,1,0:T(8,128)(2,1)S(1)} all-to-all(bf16[8,32,1536]{2,1,0:T(8,128)(2,1)S(1)} %flip_in.1.gated_ref), channel_id=1, replica_groups=mesh['seq'=8,'mp'=4] {'seq'}, dimensions={0} | all-to-all | bytes 1572864 | tf_op jit(solution)/shard_map/all_to_all | solution.py:272
  31.5 11.7 %conv.1 = bf16[8,32,1024]{2,1,0:T(8,128)(2,1)} custom-call(bf16[8,32,1536]{2,1,0:T(8,128)(2,1)S(1)} %all_to_all.10.refs_0_), custom_call_target="tpu_custom_call" | custom-call | flops 2281701376 | tf_op jit(solution)/shard_map/conv/pallas_call | solution.py:202
  43.1 0.0 copy-start
  43.1 3.7 %all-to-all-start.1 = ((bf16[8,32,1024]{2,1,0:T(8,128)(2,1)}), bf16[8,32,1024]{2,1,0:T(8,128)(2,1)S(1)}, u32[]{:S(2)}, u32[]{:S(2)}) async-start(bf16[8,32,1024]{2,1,0:T(8,128)(2,1)} %conv.1), calls=%async_computation.1 | async-start | bytes 1048576 | tf_op jit(solution)/shard_map/all_to_all | solution.py:276
  46.9 0.0 copy-start.4
  46.9 0.0 copy-done
  46.9 0.7 copy-done.4
  47.5 1.0 %flip_out_gate.1 = (f32[256,128]{1,0:T(8,128)S(1)}, bf16[8,32,1024]{2,1,0:T(8,128)(2,1)S(1)}) custom-call(bf16[1024,256]{1,0:T(8,128)(2,1)S(1)} %copy-done, f32[1,256]{1,0:T(1,128)S(1)} %bitcast.1), custom_call_target="tpu_custom_call" | custom-call | flops 134217728 | tf_op jit(solution)/shard_map/flip_out_gate/pallas_call | solution.py:273
  48.5 12.5 %all-to-all-done.1.y_ref = bf16[8,32,1024]{2,1,0:T(8,128)(2,1)S(1)} async-done(((bf16[8,32,1024]{2,1,0:T(8,128)(2,1)}), bf16[8,32,1024]{2,1,0:T(8,128)(2,1)S(1)}, u32[]{:S(2)}, u32[]{:S(2)}) %all-to-all-start.1) | async-done | bytes 524320 | tf_op jit(solution)/shard_map/all_to_all | solution.py:276
  61.0 0.8 %mix.1 = (f32[8,32,1024]{2,1,0:T(8,128)S(1)}, f32[8,1024]{1,0:T(8,128)S(1)}) custom-call(bf16[8,32,1024]{2,1,0:T(8,128)(2,1)S(1)} %all-to-all-done.1.y_ref, bf16[8,32,1536]{2,1,0:T(8,128)(2,1)S(1)} %flip_in.1.gated_ref, bf16[8,32,1024]{2,1,0:T(8,128)(2,1)S(1)} %get-tuple-element.9.og_ref, f32[256,128]{1,0:T(8,128)S(1)} %get-tuple-element.10.column_ref), custom_call_target="tpu_custom_call" | custom-call | flops 2097152 | tf_op jit(solution)/shard_map/mix/pallas_call | solution.py:280
  61.9 0.1 collective-permute-start.2
  62.0 1.6 %collective-permute-start.1 = (f32[1,1024]{1,0:T(1,128)S(1)}, f32[1,1024]{1,0:T(1,128)S(1)}, u32[]{:S(2)}, u32[]{:S(2)}) collective-permute-start(f32[1,1024]{1,0:T(1,128)S(1)} %slice.2), channel_id=1, source_target_pairs={{0,2},{1,3},{2,0},{3,1},{4,6},{5,7},{6,4},{7,5},{8,10},{9,11},{10,... | collective-permute-start | bytes 12296 | tf_op jit(solution)/shard_map/ppermute | solution.py:289
  63.5 0.2 collective-permute-start
  63.7 0.0 collective-permute-done.2.refs_3_
  63.7 2.0 %collective-permute-done.1.refs_2_ = f32[1,1024]{1,0:T(1,128)S(1)} collective-permute-done((f32[1,1024]{1,0:T(1,128)S(1)}, f32[1,1024]{1,0:T(1,128)S(1)}, u32[]{:S(2)}, u32[]{:S(2)}) %collective-permute-start.1) | collective-permute-done | bytes 4128 | tf_op jit(solution)/shard_map/ppermute | solution.py:289
  65.6 0.9 %collective-permute-done.refs_1_ = f32[1,1024]{1,0:T(1,128)S(1)} collective-permute-done((f32[1,1024]{1,0:T(1,128)S(1)}, f32[1,1024]{1,0:T(1,128)S(1)}, u32[]{:S(2)}, u32[]{:S(2)}) %collective-permute-start) | collective-permute-done | bytes 4128 | tf_op jit(solution)/shard_map/ppermute | solution.py:289
  66.6 1.8 %finish.1 = bf16[1024,256]{1,0:T(8,128)(2,1)} custom-call(f32[8,1024]{1,0:T(8,128)S(1)} %get-tuple-element.11.refs_0_, f32[1,1024]{1,0:T(1,128)S(1)} %collective-permute-done.refs_1_, f32[1,1024]{1,0:T(1,128)S(1)} %collective-permute-done.1.refs_2_, f32[1,1024]{1,0:T(1,128)S(1)} %collective-permute-done.2.refs_3_, f32[8,32,1024]{2,1,0:T(8,128)S(1)} %get-tuple-element.12.refs_4_), custom_call_target="tpu_custom_call" | custom-call | flops 134217728 | tf_op jit(solution)/shard_map/finish/pallas_call | solution.py:292
  (1 shorter events, 0.0 us)
Async XLA Ops:
  0.0 1.0 %copy-start.1 = (bf16[1024,256]{1,0:T(8,128)(2,1)S(1)}, bf16[1024,256]{1,0:T(8,128)(2,1)}, u32[]{:S(2)}) copy-start(bf16[1024,256]{1,0:T(8,128)(2,1)} %gate_ref.1) | copy-start | bytes 1572868
  1.0 1.0 %copy-start.2 = (bf16[1024,256]{1,0:T(8,128)(2,1)S(1)}, bf16[1024,256]{1,0:T(8,128)(2,1)}, u32[]{:S(2)}) copy-start(bf16[1024,256]{1,0:T(8,128)(2,1)} %value_ref.1) | copy-start | bytes 1572868
  2.1 0.9 %copy-start.3 = (bf16[512,256]{1,0:T(8,128)(2,1)S(1)}, bf16[512,256]{1,0:T(8,128)(2,1)}, u32[]{:S(2)}) copy-start(bf16[512,256]{1,0:T(8,128)(2,1)} %taps_ref.1) | copy-start | bytes 786436
  43.1 3.7 %copy-start = (bf16[1024,256]{1,0:T(8,128)(2,1)S(1)}, bf16[1024,256]{1,0:T(8,128)(2,1)}, u32[]{:S(2)}) copy-start(bf16[1024,256]{1,0:T(8,128)(2,1)} %og_ref.1) | copy-start | bytes 1572868
  43.1 17.9 %all-to-all-start.1 = ((bf16[8,32,1024]{2,1,0:T(8,128)(2,1)}), bf16[8,32,1024]{2,1,0:T(8,128)(2,1)S(1)}, u32[]{:S(2)}, u32[]{:S(2)}) async-start(bf16[8,32,1024]{2,1,0:T(8,128)(2,1)} %conv.1), calls=%async_computation.1 | async-start | bytes 1048576 | tf_op jit(solution)/shard_map/all_to_all | solution.py:276
  46.9 0.7 copy-start.4
  61.9 1.8 %collective-permute-start.2 = (f32[1,1024]{1,0:T(1,128)S(1)}, f32[1,1024]{1,0:T(1,128)S(1)}, u32[]{:S(2)}, u32[]{:S(2)}) collective-permute-start(f32[1,1024]{1,0:T(1,128)S(1)} %slice.2), channel_id=1, source_target_pairs={{0,3},{1,0},{2,1},{3,2},{4,7},{5,4},{6,5},{7,6},{8,11},{9,8},{10,9... | collective-permute-start | bytes 12296 | tf_op jit(solution)/shard_map/ppermute | solution.py:289
  62.0 3.7 %collective-permute-start.1 = (f32[1,1024]{1,0:T(1,128)S(1)}, f32[1,1024]{1,0:T(1,128)S(1)}, u32[]{:S(2)}, u32[]{:S(2)}) collective-permute-start(f32[1,1024]{1,0:T(1,128)S(1)} %slice.2), channel_id=1, source_target_pairs={{0,2},{1,3},{2,0},{3,1},{4,6},{5,7},{6,4},{7,5},{8,10},{9,11},{10,... | collective-permute-start | bytes 12296 | tf_op jit(solution)/shard_map/ppermute | solution.py:289
  63.5 3.0 %collective-permute-start = (f32[1,1024]{1,0:T(1,128)S(1)}, f32[1,1024]{1,0:T(1,128)S(1)}, u32[]{:S(2)}, u32[]{:S(2)}) collective-permute-start(f32[1,1024]{1,0:T(1,128)S(1)} %slice.2), channel_id=1, source_target_pairs={{0,1},{1,2},{2,3},{3,0},{4,5},{5,6},{6,7},{7,4},{8,9},{9,10},{10,1... | collective-permute-start | bytes 12296 | tf_op jit(solution)/shard_map/ppermute | solution.py:289

commit v3 on v2

--- a/solution.py
+++ b/solution.py
@@ -1,4 +1,5 @@
 import functools
+import math
 
 import jax
 import jax.numpy as jnp
@@ -16,13 +17,16 @@
 NT = (((1,), (1,)), ((), ()))
 
 
-def vmem_call(body, out_shape, scratch=(), flops=0, name=None, limit=6, inputs=1):
-    spec = pl.BlockSpec(memory_space=pltpu.VMEM)
+def vmem_call(
+    body, out_shape, scratch=(), flops=0, name=None, limit=6, inputs=1, fetch=False, store=False
+):
+    spec, placed = pl.BlockSpec(memory_space=pltpu.VMEM), pl.BlockSpec(memory_space=pltpu.HBM)
+    out_spec = placed if store else spec
     return pl.pallas_call(
         body,
         out_shape=out_shape,
-        in_specs=[spec] * inputs,
-        out_specs=[spec] * len(out_shape) if isinstance(out_shape, (list, tuple)) else spec,
+        in_specs=[placed if fetch else spec] * inputs,
+        out_specs=[out_spec] * len(out_shape) if isinstance(out_shape, (list, tuple)) else out_spec,
         scratch_shapes=list(scratch),
         compiler_params=pltpu.CompilerParams(vmem_limit_bytes=limit << 20),
         cost_estimate=pl.CostEstimate(flops=flops, bytes_accessed=0, transcendentals=0),
@@ -48,18 +52,33 @@
             ref[owner, :, span] = flipped[at : at + part, :]
 
 
-def flip_in(gate_ref, value_ref, taps_ref, *out_refs):
-    unit = unit_matrix(gate_ref.shape[1])
+def flip_in(gate_hbm, value_hbm, taps_hbm, *refs):
+    out_refs, (gate_ref, value_ref, taps_ref, sems) = refs[:-4], refs[-4:]
     tokens = gate_ref.shape[0]
     step = min(WIDE, tokens)
+    steps = tokens // step
+
+    def arrive(source, target, lane, i):
+        rows = pl.ds(i * step if isinstance(i, int) else pl.multiple_of(i * step, step), step)
+        return pltpu.make_async_copy(source.at[rows, :], target.at[rows, :], sems.at[lane, i])
+
+    for i in range(steps):
+        arrive(gate_hbm, gate_ref, 0, i).start()
+        arrive(value_hbm, value_ref, 1, i).start()
+    rest = pltpu.make_async_copy(taps_hbm, taps_ref, sems.at[2, 0])
+    rest.start()
+    unit = unit_matrix(gate_ref.shape[1])
 
     def some(i, carry):
         rows = pl.ds(pl.multiple_of(i * step, step), step)
+        arrive(gate_hbm, gate_ref, 0, i).wait()
+        arrive(value_hbm, value_ref, 1, i).wait()
         gated = (gate_ref[rows, :].astype(F32) * value_ref[rows, :].astype(F32)).astype(BF16)
         deal(flip(gated, unit), out_refs, rows)
         return carry
 
-    lax.fori_loop(0, tokens // step, some, 0)
+    lax.fori_loop(0, steps, some, 0)
+    rest.wait()
     deal(flip(taps_ref[...], unit), out_refs, pl.ds(tokens, taps_ref.shape[0]))
 
 
@@ -76,7 +95,7 @@
     column_ref[...] = jnp.broadcast_to(skip_ref[...], (LANES, skip_ref.shape[1])).T
 
 
-UNROLL = 2
+UNROLL = 8
 PACK = 16
 
 def conv_body(*refs):
@@ -91,6 +110,7 @@
     h_blocks = h_sources * h_per
     rows = 2 * blocks
     pitch = channels + 8
+    each = math.gcd(UNROLL, channels)
     low = lax.broadcasted_iota(jnp.int32, (channels, LANES), 1) < HALF
     zero = jnp.zeros((channels, LANES), F32)
 
@@ -119,33 +139,25 @@
 
     lax.fori_loop(0, h_sources, spread_taps, 0)
 
-    lane = lax.broadcasted_iota(jnp.int32, (PACK, LANES), 1)
-    row = lax.broadcasted_iota(jnp.int32, (PACK, LANES), 0)
+    lane = lax.broadcasted_iota(jnp.int32, (HALF, LANES), 1)
+    row = lax.broadcasted_iota(jnp.int32, (HALF, LANES), 0)
     ahead = lane >= row
-    lane16 = lane.astype(F32).astype(BF16)
 
     def channel(c):
         v = vs[pl.ds(c, rows, stride=pitch), :]
         even = v.astype(BF16)
         odd = jnp.concatenate([jnp.zeros((8, LANES), F32), v[:-8]], axis=0).astype(BF16)
-        before = jnp.zeros((PACK, LANES), F32)
-        turns = [jnp.zeros((PACK, LANES), BF16)] * (HALF // PACK)
+        before = jnp.zeros((HALF, LANES), F32)
         tiles = []
         z = None
         for m in range(h_blocks + 1):
             if m < h_blocks:
-                line = jnp.broadcast_to(hs[pl.ds(m * pitch + c, 1), :], (PACK, LANES))
+                line = jnp.broadcast_to(hs[pl.ds(m * pitch + c, 1), :], (HALF, LANES))
                 now = pltpu.roll(line, 0, 1, stride=1, stride_axis=0)
             else:
-                now = jnp.zeros((PACK, LANES), F32)
-            base = jnp.where(ahead, now, before).astype(BF16)
+                now = jnp.zeros((HALF, LANES), F32)
+            tiles.append(jnp.where(ahead, now, before).astype(BF16))
             before = now
-            group = [base]
-            for q in range(1, HALF // PACK):
-                turned = pltpu.roll(base, PACK * q, 1)
-                group.append(jnp.where(lane16 >= PACK * q, turned, turns[q]))
-                turns[q] = turned
-            tiles.append(jnp.concatenate(group, axis=0))
             if m % 8 == 7 or m == h_blocks:
                 k = m // 8
                 top = PACK * k
@@ -166,11 +178,11 @@
         zs1[pl.ds(c, rows, stride=pitch), :] = z[:, LANES:]
 
     def group(g, carry):
-        for i in range(UNROLL):
-            channel(g * UNROLL + i)
-        return carry
-
-    lax.fori_loop(0, channels // UNROLL, group, 0)
+        for i in range(each):
+            channel(g * each + i)
+        return carry
+
+    lax.fori_loop(0, channels // each, group, 0)
 
     def gather(s, carry):
         late1, late2, late22 = carry
@@ -234,10 +246,15 @@
 
 
 def finish(total, peers, *refs):
-    powers, mixed, out_ref = refs[:peers], refs[peers:-1], refs[-1]
+    powers, mixed, (out_hbm, out_ref, sems) = refs[:peers], refs[peers:-3], refs[-3:]
     step = min(WIDE, out_ref.shape[0])
+    steps = out_ref.shape[0] // step
     unit = unit_matrix(step)
     owners = mixed[0].shape[0]
+
+    def leave(i):
+        rows = pl.ds(i * step if isinstance(i, int) else pl.multiple_of(i * step, step), step)
+        return pltpu.make_async_copy(out_ref.at[rows, :], out_hbm.at[rows, :], sems.at[i])
 
     def some(i, carry):
         rows = pl.ds(pl.multiple_of(i * step, step), step)
@@ -249,9 +266,12 @@
             (ref[owner, :, rows] * scale).astype(BF16) for owner in range(owners) for ref in mixed
         ]
         out_ref[rows, :] = flip(jnp.concatenate(pieces, axis=0), unit)
-        return carry
-
-    lax.fori_loop(0, out_ref.shape[0] // step, some, 0)
+        leave(i).start()
+        return carry
+
+    lax.fori_loop(0, steps, some, 0)
+    for i in range(steps):
+        leave(i).wait()
 
 
 def local(n_seq, n_mp, gate_in, value_in, out_gate, filter_taps, skip_gain):
@@ -267,7 +287,19 @@
     flat = [jax.ShapeDtypeStruct((n_seq, part, tokens), F32), jax.ShapeDtypeStruct((8, tokens), F32)]
     product = 2 * channels * channels
     both = vmem_call(
-        flip_in, dealt_both, name="flip_in", flops=product * (tokens + taps), inputs=3
+        flip_in,
+        dealt_both,
+        [
+            pltpu.VMEM((tokens, channels), BF16),
+            pltpu.VMEM((tokens, channels), BF16),
+            pltpu.VMEM((taps, channels), BF16),
+            pltpu.SemaphoreType.DMA((3, max(1, tokens // WIDE))),
+        ],
+        name="flip_in",
+        flops=product * (tokens + taps),
+        inputs=3,
+        fetch=True,
+        limit=60,
     )(gate_in, value_in, filter_taps)
     moved = [swap(piece) for piece in both]
     skip, *og = vmem_call(
@@ -292,9 +324,11 @@
     return vmem_call(
         functools.partial(finish, channels * n_mp, n_mp),
         jax.ShapeDtypeStruct((tokens, channels), BF16),
+        [pltpu.VMEM((tokens, channels), BF16), pltpu.SemaphoreType.DMA((max(1, tokens // WIDE),))],
         name="finish",
         flops=2 * channels * tokens * WIDE,
         inputs=n_mp + chunks,
+        store=True,
     )(*powers, *mixed)
 
 

time: 68.7 us -> 64.2 us (0.934)
  local copies, waits for them, and re-layouts: 3.71 us -> 0.68 us
  Pallas kernels: 16.5 us -> 14.8 us
    pallas_call x1, Pallas kernels: 11.7 us -> 8.14 us  [convolve(): vmem_call(conv_body, jax.ShapeDtypeStruct((sources, channels, span), BF16...]
    unnamed x10 -> x6, local copies, waits for them, and re-layouts: 3.7 us -> 0.67 us
    pallas_call x1, Pallas kernels: 1.17 us -> 3.13 us  [local(): vmem_call(flip_in, dealt_both, [pltpu.VMEM((tokens, channels), BF16), plt...]
  transfers between devices with their start and end apart: 4 -> 4, of which waited for: 3 -> 3; matrix products, arithmetic and copies ran while one was open for 0% -> 0% of each run, Pallas kernels for 1% -> 2%
where the time goes in v3:
time: 64.2 us; the launch traced here: 63.9 us
  blocking collectives  27.5 us (43%)
  waiting for transfers between devices  15.4 us (24%)
  Pallas kernels  14.8 us (23%)
  starting transfers between devices  5.5 us (9%)
  local copies, waits for them, and re-layouts  0.68 us (1%)
    all_to_all x1, blocking collectives, local(): moved = [swap(piece) for piece in both]  27.5 us
    all_to_all x1, waiting for transfers between devices, local(): y = [swap(convolve(piece, tokens)) for piece in moved]  12.5 us
    pallas_call x1, Pallas kernels, convolve(): vmem_call(conv_body, jax.ShapeDtypeStruct((sources, channels, span), BF16...  8.14 us
    all_to_all x1, starting transfers between devices, local(): y = [swap(convolve(piece, tokens)) for piece in moved]  3.73 us
    pallas_call x1, Pallas kernels, local(): vmem_call(flip_in, dealt_both, [pltpu.VMEM((tokens, channels), BF16), plt...  3.13 us
    ppermute x3, waiting for transfers between devices, local(): lax.ppermute(power[:1], 'mp', [(j, (j + d) % n_mp) for j in range(n_mp)])  2.88 us
    ppermute x3, starting transfers between devices, local(): lax.ppermute(power[:1], 'mp', [(j, (j + d) % n_mp) for j in range(n_mp)])  1.77 us
    pallas_call x1, Pallas kernels, local(): vmem_call(functools.partial(finish, channels * n_mp, n_mp), jax.ShapeDtyp...  1.7 us
  transfers between devices with their start and end apart: 4, of which 3 were waited for; matrix products, arithmetic and copies ran while one was open for 0% of the time, Pallas kernels for 2%

profile of v3, /device:TPU:0, one launch (start us, length us, event | category | flops | bytes accessed | tf_op | source)
XLA Modules:
  0.0 63.9 jit_solution(9236131670874170118)
XLA Ops:
  0.0 3.1 %flip_in.1.gated_ref = bf16[8,32,1536]{2,1,0:T(8,128)(2,1)} custom-call(bf16[1024,256]{1,0:T(8,128)(2,1)} %gate_hbm.1, bf16[1024,256]{1,0:T(8,128)(2,1)} %value_hbm.1, bf16[512,256]{1,0:T(8,128)(2,1)} %taps_hbm.1), custom_call_target="tpu_custom_call" | custom-call | flops 201326592 | tf_op jit(solution)/shard_map/flip_in/pallas_call | solution.py:289
  3.1 27.5 %all_to_all.10.refs_0_ = bf16[8,32,1536]{2,1,0:T(8,128)(2,1)S(1)} all-to-all(bf16[8,32,1536]{2,1,0:T(8,128)(2,1)} %flip_in.1.gated_ref), channel_id=1, replica_groups=mesh['seq'=8,'mp'=4] {'seq'}, dimensions={0} | all-to-all | bytes 1572864 | tf_op jit(solution)/shard_map/all_to_all | solution.py:304
  30.6 0.0 copy-start.1
  30.6 8.1 %conv.1 = bf16[8,32,1024]{2,1,0:T(8,128)(2,1)} custom-call(bf16[8,32,1536]{2,1,0:T(8,128)(2,1)S(1)} %all_to_all.10.refs_0_), custom_call_target="tpu_custom_call" | custom-call | flops 2281701376 | tf_op jit(solution)/shard_map/conv/pallas_call | solution.py:214
  38.7 0.0 copy-start
  38.7 3.7 %all-to-all-start.1 = ((bf16[8,32,1024]{2,1,0:T(8,128)(2,1)}), bf16[8,32,1024]{2,1,0:T(8,128)(2,1)S(1)}, u32[]{:S(2)}, u32[]{:S(2)}) async-start(bf16[8,32,1024]{2,1,0:T(8,128)(2,1)} %conv.1), calls=%async_computation.1 | async-start | bytes 1048576 | tf_op jit(solution)/shard_map/all_to_all | solution.py:308
  42.5 0.0 copy-start.2
  42.5 0.0 copy-done.1
  42.5 0.7 %copy-done.2 = f32[256]{0:T(256)S(1)} copy-done((f32[256]{0:T(256)S(1)}, f32[256]{0:T(256)}, u32[]{:S(2)}) %copy-start.2) | copy-done | bytes 1048
  43.1 1.0 %flip_out_gate.1 = (f32[256,128]{1,0:T(8,128)S(1)}, bf16[8,32,1024]{2,1,0:T(8,128)(2,1)S(1)}) custom-call(bf16[1024,256]{1,0:T(8,128)(2,1)S(1)} %copy-done.1, f32[1,256]{1,0:T(1,128)S(1)} %bitcast.1), custom_call_target="tpu_custom_call" | custom-call | flops 134217728 | tf_op jit(solution)/shard_map/flip_out_gate/pallas_call | solution.py:305
  44.1 12.5 %all-to-all-done.1.y_ref = bf16[8,32,1024]{2,1,0:T(8,128)(2,1)S(1)} async-done(((bf16[8,32,1024]{2,1,0:T(8,128)(2,1)}), bf16[8,32,1024]{2,1,0:T(8,128)(2,1)S(1)}, u32[]{:S(2)}, u32[]{:S(2)}) %all-to-all-start.1) | async-done | bytes 524320 | tf_op jit(solution)/shard_map/all_to_all | solution.py:308
  56.6 0.0 copy-done
  56.6 0.8 %mix.1 = (f32[8,32,1024]{2,1,0:T(8,128)S(1)}, f32[8,1024]{1,0:T(8,128)S(1)}) custom-call(bf16[8,32,1024]{2,1,0:T(8,128)(2,1)S(1)} %all-to-all-done.1.y_ref, bf16[8,32,1536]{2,1,0:T(8,128)(2,1)S(1)} %copy-done, bf16[8,32,1024]{2,1,0:T(8,128)(2,1)S(1)} %get-tuple-element.9.og_ref, f32[256,128]{1,0:T(8,128)S(1)} %get-tuple-element.10.column_ref), custom_call_target="tpu_custom_call" | custom-call | flops 2097152 | tf_op jit(solution)/shard_map/mix/pallas_call | solution.py:312
  57.5 0.1 collective-permute-start.2
  57.6 1.6 %collective-permute-start.1 = (f32[1,1024]{1,0:T(1,128)S(1)}, f32[1,1024]{1,0:T(1,128)S(1)}, u32[]{:S(2)}, u32[]{:S(2)}) collective-permute-start(f32[1,1024]{1,0:T(1,128)S(1)} %slice.2), channel_id=1, source_target_pairs={{0,2},{1,3},{2,0},{3,1},{4,6},{5,7},{6,4},{7,5},{8,10},{9,11},{10,... | collective-permute-start | bytes 12296 | tf_op jit(solution)/shard_map/ppermute | solution.py:321
  59.1 0.2 collective-permute-start
  59.3 0.0 collective-permute-done.2.refs_3_
  59.3 2.0 %collective-permute-done.1.refs_2_ = f32[1,1024]{1,0:T(1,128)S(1)} collective-permute-done((f32[1,1024]{1,0:T(1,128)S(1)}, f32[1,1024]{1,0:T(1,128)S(1)}, u32[]{:S(2)}, u32[]{:S(2)}) %collective-permute-start.1) | collective-permute-done | bytes 4128 | tf_op jit(solution)/shard_map/ppermute | solution.py:321
  61.2 0.9 %collective-permute-done.refs_1_ = f32[1,1024]{1,0:T(1,128)S(1)} collective-permute-done((f32[1,1024]{1,0:T(1,128)S(1)}, f32[1,1024]{1,0:T(1,128)S(1)}, u32[]{:S(2)}, u32[]{:S(2)}) %collective-permute-start) | collective-permute-done | bytes 4128 | tf_op jit(solution)/shard_map/ppermute | solution.py:321
  62.2 1.7 %finish.1 = bf16[1024,256]{1,0:T(8,128)(2,1)} custom-call(f32[8,1024]{1,0:T(8,128)S(1)} %get-tuple-element.11.refs_0_, f32[1,1024]{1,0:T(1,128)S(1)} %collective-permute-done.refs_1_, f32[1,1024]{1,0:T(1,128)S(1)} %collective-permute-done.1.refs_2_, f32[1,1024]{1,0:T(1,128)S(1)} %collective-permute-done.2.refs_3_, f32[8,32,1024]{2,1,0:T(8,128)S(1)} %get-tuple-element.12.refs_4_), custom_call_target="tpu_custom_call" | custom-call | flops 134217728 | tf_op jit(solution)/shard_map/finish/pallas_call | solution.py:324
  (1 shorter events, 0.0 us)
Async XLA Ops:
  30.6 11.9 %copy-start.1 = (bf16[1024,256]{1,0:T(8,128)(2,1)S(1)}, bf16[1024,256]{1,0:T(8,128)(2,1)}, u32[]{:S(2)}) copy-start(bf16[1024,256]{1,0:T(8,128)(2,1)} %og_ref.1) | copy-start | bytes 1572868
  38.7 17.9 %copy-start = (bf16[8,32,1536]{2,1,0:T(8,128)(2,1)S(1)}, bf16[8,32,1536]{2,1,0:T(8,128)(2,1)}, u32[]{:S(2)}) copy-start(bf16[8,32,1536]{2,1,0:T(8,128)(2,1)} %flip_in.1.gated_ref) | copy-start | bytes 2359300
  38.7 17.9 %all-to-all-start.1 = ((bf16[8,32,1024]{2,1,0:T(8,128)(2,1)}), bf16[8,32,1024]{2,1,0:T(8,128)(2,1)S(1)}, u32[]{:S(2)}, u32[]{:S(2)}) async-start(bf16[8,32,1024]{2,1,0:T(8,128)(2,1)} %conv.1), calls=%async_computation.1 | async-start | bytes 1048576 | tf_op jit(solution)/shard_map/all_to_all | solution.py:308
  42.5 0.7 %copy-start.2 = (f32[256]{0:T(256)S(1)}, f32[256]{0:T(256)}, u32[]{:S(2)}) copy-start(f32[256]{0:T(256)} %param.9) | copy-start | bytes 3076
  57.5 1.8 %collective-permute-start.2 = (f32[1,1024]{1,0:T(1,128)S(1)}, f32[1,1024]{1,0:T(1,128)S(1)}, u32[]{:S(2)}, u32[]{:S(2)}) collective-permute-start(f32[1,1024]{1,0:T(1,128)S(1)} %slice.2), channel_id=1, source_target_pairs={{0,3},{1,0},{2,1},{3,2},{4,7},{5,4},{6,5},{7,6},{8,11},{9,8},{10,9... | collective-permute-start | bytes 12296 | tf_op jit(solution)/shard_map/ppermute | solution.py:321
  57.6 3.7 %collective-permute-start.1 = (f32[1,1024]{1,0:T(1,128)S(1)}, f32[1,1024]{1,0:T(1,128)S(1)}, u32[]{:S(2)}, u32[]{:S(2)}) collective-permute-start(f32[1,1024]{1,0:T(1,128)S(1)} %slice.2), channel_id=1, source_target_pairs={{0,2},{1,3},{2,0},{3,1},{4,6},{5,7},{6,4},{7,5},{8,10},{9,11},{10,... | collective-permute-start | bytes 12296 | tf_op jit(solution)/shard_map/ppermute | solution.py:321
  59.1 3.0 %collective-permute-start = (f32[1,1024]{1,0:T(1,128)S(1)}, f32[1,1024]{1,0:T(1,128)S(1)}, u32[]{:S(2)}, u32[]{:S(2)}) collective-permute-start(f32[1,1024]{1,0:T(1,128)S(1)} %slice.2), channel_id=1, source_target_pairs={{0,1},{1,2},{2,3},{3,0},{4,5},{5,6},{6,7},{7,4},{8,9},{9,10},{10,1... | collective-permute-start | bytes 12296 | tf_op jit(solution)/shard_map/ppermute | solution.py:321

commit v4 on v3

--- a/solution.py
+++ b/solution.py
@@ -52,34 +52,47 @@
             ref[owner, :, span] = flipped[at : at + part, :]
 
 
-def flip_in(gate_hbm, value_hbm, taps_hbm, *refs):
-    out_refs, (gate_ref, value_ref, taps_ref, sems) = refs[:-4], refs[-4:]
-    tokens = gate_ref.shape[0]
+def flip_in(gate_hbm, value_hbm, taps_hbm, out_hbm, gate_ref, value_ref, taps_ref, out_ref, sems):
+    tokens, taps = gate_ref.shape[0], taps_ref.shape[0]
     step = min(WIDE, tokens)
     steps = tokens // step
 
+    def part(i):
+        return pl.ds(i * step if isinstance(i, int) else pl.multiple_of(i * step, step), step)
+
     def arrive(source, target, lane, i):
-        rows = pl.ds(i * step if isinstance(i, int) else pl.multiple_of(i * step, step), step)
-        return pltpu.make_async_copy(source.at[rows, :], target.at[rows, :], sems.at[lane, i])
-
+        return pltpu.make_async_copy(source.at[part(i), :], target.at[part(i), :], sems.at[lane, i])
+
+    def leave(span, lane, i):
+        return pltpu.make_async_copy(
+            out_ref.at[:, :, span], out_hbm.at[:, :, span], sems.at[lane, i]
+        )
+
+    rest = pltpu.make_async_copy(taps_hbm, taps_ref, sems.at[3, 0])
+    rest.start()
     for i in range(steps):
         arrive(gate_hbm, gate_ref, 0, i).start()
         arrive(value_hbm, value_ref, 1, i).start()
-    rest = pltpu.make_async_copy(taps_hbm, taps_ref, sems.at[2, 0])
-    rest.start()
     unit = unit_matrix(gate_ref.shape[1])
+    behind = pl.ds(tokens, taps)
+    rest.wait()
+    deal(flip(taps_ref[...], unit), (out_ref,), behind)
+    last = leave(behind, 4, 0)
+    last.start()
 
     def some(i, carry):
-        rows = pl.ds(pl.multiple_of(i * step, step), step)
         arrive(gate_hbm, gate_ref, 0, i).wait()
         arrive(value_hbm, value_ref, 1, i).wait()
+        rows = part(i)
         gated = (gate_ref[rows, :].astype(F32) * value_ref[rows, :].astype(F32)).astype(BF16)
-        deal(flip(gated, unit), out_refs, rows)
-        return carry
-
-    lax.fori_loop(0, steps, some, 0)
-    rest.wait()
-    deal(flip(taps_ref[...], unit), out_refs, pl.ds(tokens, taps_ref.shape[0]))
+        deal(flip(gated, unit), (out_ref,), rows)
+        leave(rows, 2, i).start()
+        return carry
+
+    lax.fori_loop(0, steps, some, 0, unroll=UNROLL_IN)
+    for i in range(steps):
+        leave(part(i), 2, i).wait()
+    last.wait()
 
 
 def flip_out_gate(og_ref, skip_ref, column_ref, *out_refs):
@@ -96,11 +109,12 @@
 
 
 UNROLL = 8
+UNROLL_IN = 1
 PACK = 16
 
 def conv_body(*refs):
-    x_ref, h_ref = refs[0], refs[-6]
-    y_ref, vs, hs, zs0, zs1 = refs[-5:]
+    x_ref, h_ref = refs[0], refs[-8]
+    y_hbm, y_ref, vs, hs, zs0, zs1, sems = refs[-7:]
     sources, channels, span = y_ref.shape
     per_source = span // LANES
     blocks = sources * per_source
@@ -128,7 +142,7 @@
             older, old = old, (x, turned)
         return older, old
 
-    lax.fori_loop(0, sources, spread, ((zero, zero), (zero, zero)))
+    lax.fori_loop(0, sources, spread, ((zero, zero), (zero, zero)), unroll=4)
 
     def spread_taps(s, carry):
         for b in range(h_per):
@@ -184,6 +198,9 @@
 
     lax.fori_loop(0, channels // each, group, 0)
 
+    def leave(s):
+        return pltpu.make_async_copy(y_ref.at[s], y_hbm.at[s], sems.at[s])
+
     def gather(s, carry):
         late1, late2, late22 = carry
         for b in range(per_source):
@@ -193,9 +210,16 @@
             late1 = zs1[place(s, b, 0), :] + jnp.where(low, first, second)
             late22, late2 = late2, jnp.where(low, second, 0.0)
             y_ref[s, :, pl.ds(b * LANES, LANES)] = y.astype(BF16)
+        leave(s).start()
         return late1, late2, late22
 
-    lax.fori_loop(0, sources, gather, (zero, zero, zero))
+    lax.fori_loop(0, sources, gather, (zero, zero, zero), unroll=4)
+
+    def left(s, carry):
+        leave(s).wait()
+        return carry
+
+    lax.fori_loop(0, sources, left, 0)
 
 
 def convolve(data, span):
@@ -206,11 +230,13 @@
         inputs.append(jnp.moveaxis(data[:, :, span:], 0, 1).reshape(1, channels, taps))
     blocks = sources * span // LANES
     scratch = [
+        pltpu.VMEM((sources, channels, span), BF16),
         pltpu.VMEM((2 * blocks * (channels + 8), LANES), F32),
         pltpu.VMEM((taps // LANES * (channels + 8), LANES), F32),
         pltpu.VMEM((2 * blocks * (channels + 8), LANES), F32),
         pltpu.VMEM((2 * blocks * (channels + 8), LANES), F32),
     ]
+    scratch.append(pltpu.SemaphoreType.DMA((sources,)))
     return vmem_call(
         conv_body,
         jax.ShapeDtypeStruct((sources, channels, span), BF16),
@@ -219,6 +245,7 @@
         name="conv",
         limit=28,
         inputs=len(inputs),
+        store=True,
     )(*inputs)
 
 
@@ -269,9 +296,13 @@
         leave(i).start()
         return carry
 
-    lax.fori_loop(0, steps, some, 0)
+    lax.fori_loop(0, steps, some, 0, unroll=4)
     for i in range(steps):
         leave(i).wait()
+
+
+def partner(j, d, count):
+    return (j + d) % count if count & (count - 1) else j ^ d
 
 
 def local(n_seq, n_mp, gate_in, value_in, out_gate, filter_taps, skip_gain):
@@ -286,21 +317,25 @@
     column = jax.ShapeDtypeStruct((channels, LANES), F32)
     flat = [jax.ShapeDtypeStruct((n_seq, part, tokens), F32), jax.ShapeDtypeStruct((8, tokens), F32)]
     product = 2 * channels * channels
-    both = vmem_call(
-        flip_in,
-        dealt_both,
-        [
-            pltpu.VMEM((tokens, channels), BF16),
-            pltpu.VMEM((tokens, channels), BF16),
-            pltpu.VMEM((taps, channels), BF16),
-            pltpu.SemaphoreType.DMA((3, max(1, tokens // WIDE))),
-        ],
-        name="flip_in",
-        flops=product * (tokens + taps),
-        inputs=3,
-        fetch=True,
-        limit=60,
-    )(gate_in, value_in, filter_taps)
+    both = [
+        vmem_call(
+            flip_in,
+            dealt_both[0],
+            [
+                pltpu.VMEM((tokens, channels), BF16),
+                pltpu.VMEM((tokens, channels), BF16),
+                pltpu.VMEM((taps, channels), BF16),
+                pltpu.VMEM(dealt_both[0].shape, BF16),
+                pltpu.SemaphoreType.DMA((5, max(1, tokens // WIDE))),
+            ],
+            name="flip_in",
+            flops=product * (tokens + taps),
+            inputs=3,
+            fetch=True,
+            store=True,
+            limit=60,
+        )(gate_in, value_in, filter_taps)
+    ]
     moved = [swap(piece) for piece in both]
     skip, *og = vmem_call(
         flip_out_gate, [column] + dealt, name="flip_out_gate", flops=product * tokens, inputs=2
@@ -318,7 +353,7 @@
         )(y[k], both[k], og[k], skip, *before)
         mixed.append(piece)
     powers = [power] + [
-        lax.ppermute(power[:1], "mp", [(j, (j + d) % n_mp) for j in range(n_mp)])
+        lax.ppermute(power[:1], "mp", [(j, partner(j, d, n_mp)) for j in range(n_mp)])
         for d in range(1, n_mp)
     ]
     return vmem_call(

time: 64.2 us -> 61.6 us (0.960)
  Pallas kernels: 14.8 us -> 13.1 us
  waiting for transfers between devices: 15.4 us -> 14.3 us
    ppermute x3, waiting for transfers between devices: 2.88 us -> 1.83 us  [local(): lax.ppermute(power[:1], 'mp', [(j, partner(j, d, n_mp)) for j in range(n_...]
    pallas_call x1, Pallas kernels: 8.14 us -> 7.2 us  [convolve(): vmem_call(conv_body, jax.ShapeDtypeStruct((sources, channels, span), BF16...]
where the time goes in v4:
time: 61.6 us; the launch traced here: 61.3 us
  blocking collectives  27.5 us (45%)
  waiting for transfers between devices  14.3 us (23%)
  Pallas kernels  13.1 us (21%)
  starting transfers between devices  5.66 us (9%)
  local copies, waits for them, and re-layouts  0.68 us (1%)
    all_to_all x1, blocking collectives, local(): moved = [swap(piece) for piece in both]  27.5 us
    all_to_all x1, waiting for transfers between devices, local(): y = [swap(convolve(piece, tokens)) for piece in moved]  12.5 us
    pallas_call x1, Pallas kernels, convolve(): vmem_call(conv_body, jax.ShapeDtypeStruct((sources, channels, span), BF16...  7.2 us
    all_to_all x1, starting transfers between devices, local(): y = [swap(convolve(piece, tokens)) for piece in moved]  3.74 us
    pallas_call x1, Pallas kernels, local(): vmem_call(flip_in, dealt_both[0], [pltpu.VMEM((tokens, channels), BF16),...  2.97 us
    ppermute x3, starting transfers between devices, local(): lax.ppermute(power[:1], 'mp', [(j, partner(j, d, n_mp)) for j in range(n_...  1.92 us
    ppermute x3, waiting for transfers between devices, local(): lax.ppermute(power[:1], 'mp', [(j, partner(j, d, n_mp)) for j in range(n_...  1.83 us
  transfers between devices with their start and end apart: 4, of which 3 were waited for; matrix products, arithmetic and copies ran while one was open for 0% of the time, Pallas kernels for 2%

profile of v4, /device:TPU:0, one launch (start us, length us, event | category | flops | bytes accessed | tf_op | source)
XLA Modules:
  0.0 61.3 jit_solution(17202977630664838679)
XLA Ops:
  0.0 3.0 %flip_in.1.gated_ref = bf16[8,32,1536]{2,1,0:T(8,128)(2,1)} custom-call(bf16[1024,256]{1,0:T(8,128)(2,1)} %gate_hbm.1, bf16[1024,256]{1,0:T(8,128)(2,1)} %value_hbm.1, bf16[512,256]{1,0:T(8,128)(2,1)} %taps_hbm.1), custom_call_target="tpu_custom_call" | custom-call | flops 201326592 | tf_op jit(solution)/shard_map/flip_in/pallas_call | solution.py:321
  3.0 27.5 %all_to_all.10.refs_0_ = bf16[8,32,1536]{2,1,0:T(8,128)(2,1)S(1)} all-to-all(bf16[8,32,1536]{2,1,0:T(8,128)(2,1)} %flip_in.1.gated_ref), channel_id=1, replica_groups=mesh['seq'=8,'mp'=4] {'seq'}, dimensions={0} | all-to-all | bytes 1572864 | tf_op jit(solution)/shard_map/all_to_all | solution.py:339
  30.4 0.0 copy-start.1
  30.4 7.2 %conv.1 = bf16[8,32,1024]{2,1,0:T(8,128)(2,1)} custom-call(bf16[8,32,1536]{2,1,0:T(8,128)(2,1)S(1)} %all_to_all.10.refs_0_), custom_call_target="tpu_custom_call" | custom-call | flops 2281701376 | tf_op jit(solution)/shard_map/conv/pallas_call | solution.py:240
  37.7 0.0 copy-start
  37.7 3.7 %all-to-all-start.1 = ((bf16[8,32,1024]{2,1,0:T(8,128)(2,1)}), bf16[8,32,1024]{2,1,0:T(8,128)(2,1)S(1)}, u32[]{:S(2)}, u32[]{:S(2)}) async-start(bf16[8,32,1024]{2,1,0:T(8,128)(2,1)} %conv.1), calls=%async_computation.1 | async-start | bytes 1048576 | tf_op jit(solution)/shard_map/all_to_all | solution.py:343
  41.4 0.0 copy-start.2
  41.4 0.0 copy-done.1
  41.4 0.7 %copy-done.2 = f32[256]{0:T(256)S(1)} copy-done((f32[256]{0:T(256)S(1)}, f32[256]{0:T(256)}, u32[]{:S(2)}) %copy-start.2) | copy-done | bytes 1048
  42.1 1.0 %flip_out_gate.1 = (f32[256,128]{1,0:T(8,128)S(1)}, bf16[8,32,1024]{2,1,0:T(8,128)(2,1)S(1)}) custom-call(bf16[1024,256]{1,0:T(8,128)(2,1)S(1)} %copy-done.1, f32[1,256]{1,0:T(1,128)S(1)} %bitcast.1), custom_call_target="tpu_custom_call" | custom-call | flops 134217728 | tf_op jit(solution)/shard_map/flip_out_gate/pallas_call | solution.py:340
  43.1 12.5 %all-to-all-done.1.y_ref = bf16[8,32,1024]{2,1,0:T(8,128)(2,1)S(1)} async-done(((bf16[8,32,1024]{2,1,0:T(8,128)(2,1)}), bf16[8,32,1024]{2,1,0:T(8,128)(2,1)S(1)}, u32[]{:S(2)}, u32[]{:S(2)}) %all-to-all-start.1) | async-done | bytes 524320 | tf_op jit(solution)/shard_map/all_to_all | solution.py:343
  55.6 0.0 copy-done
  55.6 0.8 %mix.1 = (f32[8,32,1024]{2,1,0:T(8,128)S(1)}, f32[8,1024]{1,0:T(8,128)S(1)}) custom-call(bf16[8,32,1024]{2,1,0:T(8,128)(2,1)S(1)} %all-to-all-done.1.y_ref, bf16[8,32,1536]{2,1,0:T(8,128)(2,1)S(1)} %copy-done, bf16[8,32,1024]{2,1,0:T(8,128)(2,1)S(1)} %get-tuple-element.9.og_ref, f32[256,128]{1,0:T(8,128)S(1)} %get-tuple-element.10.column_ref), custom_call_target="tpu_custom_call" | custom-call | flops 2097152 | tf_op jit(solution)/shard_map/mix/pallas_call | solution.py:347
  56.4 0.1 collective-permute-start.2
  56.5 1.6 %collective-permute-start.1 = (f32[1,1024]{1,0:T(1,128)S(1)}, f32[1,1024]{1,0:T(1,128)S(1)}, u32[]{:S(2)}, u32[]{:S(2)}) collective-permute-start(f32[1,1024]{1,0:T(1,128)S(1)} %slice.2), channel_id=1, source_target_pairs={{0,2},{1,3},{2,0},{3,1},{4,6},{5,7},{6,4},{7,5},{8,10},{9,11},{10,... | collective-permute-start | bytes 12296 | tf_op jit(solution)/shard_map/ppermute | solution.py:356
  58.1 0.3 collective-permute-start
  58.4 1.2 %collective-permute-done.2.refs_3_ = f32[1,1024]{1,0:T(1,128)S(1)} collective-permute-done((f32[1,1024]{1,0:T(1,128)S(1)}, f32[1,1024]{1,0:T(1,128)S(1)}, u32[]{:S(2)}, u32[]{:S(2)}) %collective-permute-start.2) | collective-permute-done | bytes 4128 | tf_op jit(solution)/shard_map/ppermute | solution.py:356
  59.5 0.7 %collective-permute-done.1.refs_2_ = f32[1,1024]{1,0:T(1,128)S(1)} collective-permute-done((f32[1,1024]{1,0:T(1,128)S(1)}, f32[1,1024]{1,0:T(1,128)S(1)}, u32[]{:S(2)}, u32[]{:S(2)}) %collective-permute-start.1) | collective-permute-done | bytes 4128 | tf_op jit(solution)/shard_map/ppermute | solution.py:356
  60.2 0.0 collective-permute-done.refs_1_
  60.2 1.1 %finish.1 = bf16[1024,256]{1,0:T(8,128)(2,1)} custom-call(f32[8,1024]{1,0:T(8,128)S(1)} %get-tuple-element.11.refs_0_, f32[1,1024]{1,0:T(1,128)S(1)} %collective-permute-done.refs_1_, f32[1,1024]{1,0:T(1,128)S(1)} %collective-permute-done.1.refs_2_, f32[1,1024]{1,0:T(1,128)S(1)} %collective-permute-done.2.refs_3_, f32[8,32,1024]{2,1,0:T(8,128)S(1)} %get-tuple-element.12.refs_4_), custom_call_target="tpu_custom_call" | custom-call | flops 134217728 | tf_op jit(solution)/shard_map/finish/pallas_call | solution.py:359
  (1 shorter events, 0.0 us)
Async XLA Ops:
  30.4 11.0 %copy-start.1 = (bf16[1024,256]{1,0:T(8,128)(2,1)S(1)}, bf16[1024,256]{1,0:T(8,128)(2,1)}, u32[]{:S(2)}) copy-start(bf16[1024,256]{1,0:T(8,128)(2,1)} %og_ref.1) | copy-start | bytes 1572868
  37.7 17.9 %copy-start = (bf16[8,32,1536]{2,1,0:T(8,128)(2,1)S(1)}, bf16[8,32,1536]{2,1,0:T(8,128)(2,1)}, u32[]{:S(2)}) copy-start(bf16[8,32,1536]{2,1,0:T(8,128)(2,1)} %flip_in.1.gated_ref) | copy-start | bytes 2359300
  37.7 17.9 %all-to-all-start.1 = ((bf16[8,32,1024]{2,1,0:T(8,128)(2,1)}), bf16[8,32,1024]{2,1,0:T(8,128)(2,1)S(1)}, u32[]{:S(2)}, u32[]{:S(2)}) async-start(bf16[8,32,1024]{2,1,0:T(8,128)(2,1)} %conv.1), calls=%async_computation.1 | async-start | bytes 1048576 | tf_op jit(solution)/shard_map/all_to_all | solution.py:343
  41.4 0.7 %copy-start.2 = (f32[256]{0:T(256)S(1)}, f32[256]{0:T(256)}, u32[]{:S(2)}) copy-start(f32[256]{0:T(256)} %param.9) | copy-start | bytes 3076
  56.4 3.1 %collective-permute-start.2 = (f32[1,1024]{1,0:T(1,128)S(1)}, f32[1,1024]{1,0:T(1,128)S(1)}, u32[]{:S(2)}, u32[]{:S(2)}) collective-permute-start(f32[1,1024]{1,0:T(1,128)S(1)} %slice.2), channel_id=1, source_target_pairs={{0,3},{1,2},{2,1},{3,0},{4,7},{5,6},{6,5},{7,4},{8,11},{9,10},{10,... | collective-permute-start | bytes 12296 | tf_op jit(solution)/shard_map/ppermute | solution.py:356
  56.5 3.7 %collective-permute-start.1 = (f32[1,1024]{1,0:T(1,128)S(1)}, f32[1,1024]{1,0:T(1,128)S(1)}, u32[]{:S(2)}, u32[]{:S(2)}) collective-permute-start(f32[1,1024]{1,0:T(1,128)S(1)} %slice.2), channel_id=1, source_target_pairs={{0,2},{1,3},{2,0},{3,1},{4,6},{5,7},{6,4},{7,5},{8,10},{9,11},{10,... | collective-permute-start | bytes 12296 | tf_op jit(solution)/shard_map/ppermute | solution.py:356
  58.1 2.1 %collective-permute-start = (f32[1,1024]{1,0:T(1,128)S(1)}, f32[1,1024]{1,0:T(1,128)S(1)}, u32[]{:S(2)}, u32[]{:S(2)}) collective-permute-start(f32[1,1024]{1,0:T(1,128)S(1)} %slice.2), channel_id=1, source_target_pairs={{0,1},{1,0},{2,3},{3,2},{4,5},{5,4},{6,7},{7,6},{8,9},{9,8},{10,11... | collective-permute-start | bytes 12296 | tf_op jit(solution)/shard_map/ppermute | solution.py:356
